TPU v7x, 32 devices: a 4x4x1 block of a 4x4x8 slice. The times are simulated.
32 devices in a mesh: pod: 1 (over z), dp: 4 (over y), tp: 8 (over x, core).
Axes of the slice: x: 4, y: 4, z: 1, core: 2. Of those that a mesh axis runs over, the one named last changes fastest.
The devices are a block of a 4x4x8 slice.
Arguments:
- x_saved: bfloat16 [6144, 2048], P(('pod', 'dp'))
- h_saved: bfloat16 [6144, 2048], P(('pod', 'dp'))
- mean_one: float32 [6144], P(('pod', 'dp'))
- rstd_one: float32 [6144], P(('pod', 'dp'))
- mean_two: float32 [6144], P(('pod', 'dp'))
- rstd_two: float32 [6144], P(('pod', 'dp'))
- gain_one: bfloat16 [2048], replicated
- gain_two: bfloat16 [2048], replicated
- grad_y: bfloat16 [6144, 2048], P(('pod', 'dp'))
- w_qkv: bfloat16 [2048, 3, 32, 64], P(None, None, 'tp')
- w_proj: bfloat16 [32, 64, 2048], P('tp')
- w_up: bfloat16 [2048, 8192], P(None, 'tp')
- w_down: bfloat16 [8192, 2048], P('tp')
Outputs:
- output 1: bfloat16 [6144, 2048], P(('pod', 'dp'))
- output 2: bfloat16 [2048, 3, 32, 64], P('pod', None, 'tp')
- output 3: bfloat16 [32, 64, 2048], P(('pod', 'tp'))
- output 4: bfloat16 [2048, 8192], P('pod', 'tp')
- output 5: bfloat16 [8192, 2048], P(('pod', 'tp'))
All inputs are finite; a program needn't handle non-finite values.
Results may differ from a plain program's by a relative error of at most 0.0192615.
Values are sent between devices in bfloat16 or wider.
A program may use at most 768 MiB of HBM per device.

v0:
```python
import math
import jax
import jax.numpy as jnp
from jax import lax
from jax.sharding import PartitionSpec as P

GELU_C = math.sqrt(2.0 / math.pi)


def layer_norm(row_vals, row_mean, row_rstd, gain_vec):
    x_hat = (row_vals.astype(jnp.float32) - row_mean[:, None]) * row_rstd[:, None]
    return x_hat, (x_hat * gain_vec.astype(jnp.float32)).astype(jnp.bfloat16)


def norm_back(d_norm, x_hat, row_rstd, gain_vec):
    scaled = d_norm * gain_vec.astype(jnp.float32)
    scaled_mean = jnp.mean(scaled, axis=-1, keepdims=True)
    proj_mean = jnp.mean(scaled * x_hat, axis=-1, keepdims=True)
    return row_rstd[:, None] * (scaled - scaled_mean - x_hat * proj_mean)


def gelu_pair(pre_act):
    pre_wide = pre_act.astype(jnp.float32)
    tanh_val = jnp.tanh(GELU_C * (pre_wide + 0.044715 * pre_wide * pre_wide * pre_wide))
    gelu_val = 0.5 * pre_wide * (1.0 + tanh_val)
    gelu_slope = 0.5 * (1.0 + tanh_val) + 0.5 * pre_wide * (1.0 - tanh_val * tanh_val) * GELU_C * (1.0 + 0.134145 * pre_wide * pre_wide)
    return gelu_val, gelu_slope


def causal_probs(q_heads, k_heads):
    tok_count = q_heads.shape[0]
    scores = jnp.einsum('qhe,khe->hqk', q_heads, k_heads, preferred_element_type=jnp.float32) * (q_heads.shape[-1] ** -0.5)
    row_ids = lax.broadcasted_iota(jnp.int32, (tok_count, tok_count), 0)
    col_ids = lax.broadcasted_iota(jnp.int32, (tok_count, tok_count), 1)
    scores = jnp.where(col_ids <= row_ids, scores, -1e30)
    shifted = jnp.exp(scores - jnp.max(scores, axis=-1, keepdims=True))
    return shifted / jnp.sum(shifted, axis=-1, keepdims=True)


def attn_grads(qkv_heads, prob_mat, prob_lo, d_attn):
    soft_scale = qkv_heads.shape[-1] ** -0.5
    dv_heads = jnp.einsum('hqk,qhe->khe', prob_lo, d_attn, preferred_element_type=jnp.float32).astype(jnp.bfloat16)
    d_probs = jnp.einsum('qhe,khe->hqk', d_attn, qkv_heads[:, 2], preferred_element_type=jnp.float32)
    d_scores = (prob_mat * (d_probs - jnp.sum(prob_mat * d_probs, axis=-1, keepdims=True)) * soft_scale).astype(jnp.bfloat16)
    dq_heads = jnp.einsum('hqk,khe->qhe', d_scores, qkv_heads[:, 1], preferred_element_type=jnp.float32).astype(jnp.bfloat16)
    dk_heads = jnp.einsum('hqk,qhe->khe', d_scores, qkv_heads[:, 0], preferred_element_type=jnp.float32).astype(jnp.bfloat16)
    return jnp.stack([dq_heads, dk_heads, dv_heads], axis=1)


def solution(mesh):
    row_spec = P(('pod', 'dp'), None)
    stat_spec = P(('pod', 'dp'))
    in_specs = (row_spec, row_spec, stat_spec, stat_spec, stat_spec, stat_spec, P(None), P(None), row_spec,
                P(None, None, 'tp', None), P('tp', None, None), P(None, 'tp'), P('tp', None))
    out_specs = (row_spec, P('pod', None, 'tp', None), P(('pod', 'tp'), None, None), P('pod', 'tp'), P(('pod', 'tp'), None))

    def local_step(x_saved, h_saved, mean_one, rstd_one, mean_two, rstd_two, gain_one, gain_two, grad_y, w_qkv, w_proj, w_up, w_down):
        hat_two, norm_two = layer_norm(h_saved, mean_two, rstd_two, gain_two)
        pre_act = jnp.dot(norm_two, w_up, preferred_element_type=jnp.float32).astype(jnp.bfloat16)
        gelu_val, gelu_slope = gelu_pair(pre_act)
        act_out = gelu_val.astype(jnp.bfloat16)
        d_act = lax.dot_general(grad_y, w_down, (((1,), (1,)), ((), ())), preferred_element_type=jnp.float32)
        d_pre = (d_act * gelu_slope).astype(jnp.bfloat16)
        grad_down = lax.dot_general(act_out, grad_y, (((0,), (0,)), ((), ())), preferred_element_type=jnp.float32)
        grad_up = lax.dot_general(norm_two, d_pre, (((0,), (0,)), ((), ())), preferred_element_type=jnp.float32)
        part_two = lax.dot_general(d_pre, w_up, (((1,), (1,)), ((), ())), preferred_element_type=jnp.float32).astype(jnp.bfloat16)
        d_norm_two = lax.psum(part_two, 'tp').astype(jnp.float32)
        d_mid = grad_y.astype(jnp.float32) + norm_back(d_norm_two, hat_two, rstd_two, gain_two)
        d_mid_lo = d_mid.astype(jnp.bfloat16)
        hat_one, norm_one = layer_norm(x_saved, mean_one, rstd_one, gain_one)
        qkv_heads = jnp.einsum('td,dche->tche', norm_one, w_qkv, preferred_element_type=jnp.float32).astype(jnp.bfloat16)
        prob_mat = causal_probs(qkv_heads[:, 0], qkv_heads[:, 1])
        prob_lo = prob_mat.astype(jnp.bfloat16)
        attn_out = jnp.einsum('hqk,khe->qhe', prob_lo, qkv_heads[:, 2], preferred_element_type=jnp.float32).astype(jnp.bfloat16)
        grad_proj = jnp.einsum('the,td->hed', attn_out, d_mid_lo, preferred_element_type=jnp.float32)
        d_attn = jnp.einsum('td,hed->the', d_mid_lo, w_proj, preferred_element_type=jnp.float32).astype(jnp.bfloat16)
        d_qkv = attn_grads(qkv_heads, prob_mat, prob_lo, d_attn)
        grad_qkv = jnp.einsum('td,tche->dche', norm_one, d_qkv, preferred_element_type=jnp.float32)
        part_one = jnp.einsum('tche,dche->td', d_qkv, w_qkv, preferred_element_type=jnp.float32).astype(jnp.bfloat16)
        d_norm_one = lax.psum(part_one, 'tp').astype(jnp.float32)
        grad_x = (d_mid + norm_back(d_norm_one, hat_one, rstd_one, gain_one)).astype(jnp.bfloat16)
        return (grad_x,
                lax.psum(grad_qkv, 'dp').astype(jnp.bfloat16),
                lax.psum(grad_proj, 'dp').astype(jnp.bfloat16),
                lax.psum(grad_up, 'dp').astype(jnp.bfloat16),
                lax.psum(grad_down, 'dp').astype(jnp.bfloat16))

    return jax.shard_map(local_step, mesh=mesh, in_specs=in_specs, out_specs=out_specs, check_vma=False)
```

profile of v0, /device:TPU:102, one launch (start us, length us, event | category | flops | bytes accessed | tf_op | source)
XLA Modules:
  0.0 777.4 jit_solution(8021141121388148250)
XLA Ops:
  7.2 0.0 copy-start
  7.2 0.1 all-reduce.5.cloned.1.call-start
  7.3 0.8 convert_element_type.103
  8.1 10.5 %convolution_convert_fusion.1 = bf16[1536,1024]{1,0:T(8,128)(2,1)S(1)} fusion(bf16[2048,1024]{1,0:T(8,128)(2,1)} %param.24, bf16[1536,2048]{1,0:T(8,128)(2,1)} %param.14, f32[2048]{0:T(1024)S(1)} %convert_element_type.103, f32[1536]{0:T(1024)} %param.17, f32[1536]{0:T(1024)} %param.18), kind=kOutput, calls=%fused_computation.56 | convolution fusion | flops 6459752448 | bytes 13651968 | tf_op jit(solution)/shard_map/dot_general | solution.py:59
  18.6 0.0 copy-start.18
  18.6 0.0 copy-start.17
  18.6 10.7 %fusion.29 = bf16[1536,1024]{1,0:T(8,128)(2,1)S(1)} fusion(bf16[1536,1024]{1,0:T(8,128)(2,1)S(1)} %convolution_convert_fusion.1, bf16[1536,2048]{1,0:T(8,128)(2,1)S(1)} %copy-done.5, bf16[1024,2048]{1,0:T(8,128)(2,1)S(1)} %copy-done.16), kind=kOutput, calls=%fused_computation.47 | convolution fusion | flops 6473908224 | bytes 16777216 | tf_op jit(solution)/shard_map/dot_general | solution.py:62
  29.3 0.0 copy-start.20
  29.3 1.7 copy-done.20
  31.0 0.0 copy-done.17
  31.0 8.6 %convolution_convert_fusion = bf16[1536,2048]{1,0:T(8,128)(2,1)} fusion(bf16[1536,1024]{1,0:T(8,128)(2,1)S(1)} %fusion.29, bf16[2048,1024]{1,0:T(8,128)(2,1)S(1)} %copy-done.17), kind=kOutput, calls=%fused_computation.40 | convolution fusion | flops 6445596672 | bytes 13631488 | tf_op jit(solution)/shard_map/dot_general | solution.py:66
  39.6 0.1 all-reduce.5.cloned.1.call-update
  39.7 0.3 all-reduce.7.cloned.1.call-start
  40.0 0.3 copy-done.9
  40.3 0.0 copy-done.10
  40.3 13.5 %fusion.87 = f32[2048,1024]{1,0:T(8,128)} fusion(bf16[1536,1024]{1,0:T(8,128)(2,1)} %copy-done.20, bf16[1536,2048]{1,0:T(8,128)(2,1)} %param.14, f32[2048]{0:T(1024)S(1)} %convert_element_type.103, f32[1536]{0:T(1024)S(1)} %copy-done.9, f32[1536]{0:T(1024)S(1)} %copy-done.10), kind=kOutput, calls=%fused_computation.93 | convolution fusion | flops 6458179584 | bytes 17846272 | tf_op jit(solution)/shard_map/dot_general | solution.py:65
  53.8 0.0 copy-start.13
  53.8 12.9 %fusion.38 = f32[1024,2048]{1,0:T(8,128)} fusion(bf16[1536,2048]{1,0:T(8,128)(2,1)} %param.21, bf16[1536,1024]{1,0:T(8,128)(2,1)S(1)} %copy-done.19), kind=kOutput, calls=%fused_computation.57 | convolution fusion | flops 6458179584 | bytes 17825792 | tf_op jit(solution)/shard_map/dot_general | solution.py:64
  66.8 0.0 copy-start.7
  66.8 0.0 copy-done.11
  66.8 0.0 copy-done.13
  66.8 7.6 fusion.89
  74.4 0.0 copy-done.7
  74.4 1.7 convert_element_type.113
  76.1 2.1 iota_compare_fusion
  78.2 22.3 %exponential_reduce_fusion = (f32[4,1536]{1,0:T(4,128)S(1)}, f32[4,1536,1536]{1,2,0:T(8,128)}) fusion(pred[1536,1536]{0,1:T(8,128)(4,1)} %iota_compare_fusion, bf16[1536,3,4,64]{0,3,2,1:T(8,128)(2,1)} %convert_element_type.113), kind=kOutput, calls=%fused_computation.11 | convolution fusion | flops 1245709824 | bytes 41705472 | tf_op jit(solution)/shard_map/sub | solution.py:36
  100.5 19.2 %all-reduce.5.cloned.1.call-done = bf16[1536,2048]{1,0:T(8,128)(2,1)} async-done(((bf16[1536,2048]{1,0:T(8,128)(2,1)}), bf16[1536,2048]{1,0:T(8,128)(2,1)}) %all-reduce.5.cloned.1.call-update) | async-done | bytes 6291472 | tf_op jit(solution)/shard_map/psum | solution.py:67
  119.7 7.7 fusion.18
  127.4 0.0 copy-start.6
  127.4 8.1 %multiply_add_fusion = f32[1536,2048]{1,0:T(8,128)S(1)} fusion(bf16[1536,2048]{1,0:T(8,128)(2,1)S(1)} %copy-done.2, bf16[1536,2048]{1,0:T(8,128)(2,1)} %param.14, bf16[1536,2048]{1,0:T(8,128)(2,1)} %param.21, f32[1536]{0:T(1024)S(1)} %get-tuple-element.15, f32[1536]{0:T(1024)S(1)} %get-tuple-element.16, f32[2048]{0:T(1024)S(1)} %convert_element_type.103, ...), kind=kLoop, calls=%fused_computation.29 | loop fusion | flops 34603008 | bytes 31490048 | tf_op jit(solution)/shard_map/add | solution.py:68
  135.5 4.5 copy-done.1
  140.1 1.9 fusion.58
  142.0 0.0 copy-start.4
  142.0 16.2 %fusion.75 = f32[4,1536,1536]{1,2,0:T(8,128)} fusion(bf16[1536,4,64]{0,2,1:T(8,128)(2,1)S(1)} %fusion.58, bf16[1536,3,4,64]{0,3,2,1:T(8,128)(2,1)} %convert_element_type.113), kind=kOutput, calls=%fused_computation.77 | convolution fusion | flops 1207959552 | bytes 39321600 | tf_op jit(solution)/shard_map/qhe,khe->hqk/dot_general | solution.py:43
  158.2 20.6 %fusion.66 = bf16[1536,1,4,64]{0,3,2,1:T(8,128)(2,1)} fusion(bf16[1536,4,64]{0,2,1:T(8,128)(2,1)} %copy-done.4, f32[4,1536]{1,0:T(4,128)S(1)} %get-tuple-element.13, pred[1536,1536]{0,1:T(8,128)(4,1)} %iota_compare_fusion, bf16[1536,3,4,64]{0,3,2,1:T(8,128)(2,1)} %convert_element_type.113), kind=kOutput, calls=%fused_computation.70 | convolution fusion | flops 2463505920 | bytes 5529600 | tf_op jit(solution)/shard_map/hqk,qhe->khe/dot_general | solution.py:42
  178.8 49.1 %fusion.69 = bf16[1536,1,4,64]{0,3,2,1:T(8,128)(2,1)} fusion(f32[4,1536,1536]{1,2,0:T(8,128)} %fusion.75, bf16[1536,3,4,64]{0,3,2,1:T(8,128)(2,1)} %convert_element_type.113, f32[4,1536,1536]{1,2,0:T(8,128)} %get-tuple-element.14, f32[4,1536]{1,0:T(4,128)S(1)} %get-tuple-element.13), kind=kOutput, calls=%fused_computation.71 | convolution fusion | flops 1274420736 | bytes 152616960 | tf_op jit(solution)/shard_map/hqk,qhe->khe/dot_general | solution.py:46
  227.9 48.9 %fusion.72 = bf16[1536,1,4,64]{0,3,2,1:T(8,128)(2,1)} fusion(f32[4,1536,1536]{1,2,0:T(8,128)} %fusion.75, bf16[1536,3,4,64]{0,3,2,1:T(8,128)(2,1)} %convert_element_type.113, f32[4,1536,1536]{1,2,0:T(8,128)} %get-tuple-element.14, f32[4,1536]{1,0:T(4,128)S(1)} %get-tuple-element.13), kind=kOutput, calls=%fused_computation.72 | convolution fusion | flops 1274420736 | bytes 152616960 | tf_op jit(solution)/shard_map/hqk,khe->qhe/dot_general | solution.py:45
  276.8 8.6 %bitcast_convert_fusion = bf16[1536,2048]{1,0:T(8,128)(2,1)} fusion(bf16[2048,3,4,64]{0,3,2,1:T(8,128)(2,1)S(1)} %copy-done, bf16[1536,1,4,64]{0,3,2,1:T(8,128)(2,1)} %fusion.66, bf16[1536,1,4,64]{0,3,2,1:T(8,128)(2,1)} %fusion.69, bf16[1536,1,4,64]{0,3,2,1:T(8,128)(2,1)} %fusion.72), kind=kOutput, calls=%fused_computation.22 | convolution fusion | flops 4837343232 | bytes 11796480 | tf_op jit(solution)/shard_map/tche,dche->td/dot_general | solution.py:79
  285.4 3.3 pad_maximum_fusion
  288.6 19.8 %fusion.34 = f32[4,64,2048]{2,1,0:T(8,128)} fusion(f32[1536,2048]{1,0:T(8,128)} %copy-done.1, bf16[1536,3,4,64]{0,3,2,1:T(8,128)(2,1)} %convert_element_type.113, f32[4,1536,1536]{1,2,0:T(8,128)} %get-tuple-element.14, f32[4,1536]{1,0:T(4,128)S(1)} %get-tuple-element.13), kind=kOutput, calls=%fused_computation.52 | convolution fusion | flops 2840985600 | bytes 53239808 | tf_op jit(solution)/shard_map/the,td->hed/dot_general | solution.py:75
  308.4 0.1 all-reduce.7.cloned.1.call-update
  308.5 0.6 copy-done.8
  309.1 0.0 copy-done.12
  309.1 0.0 copy-done.14
  309.2 9.9 %fusion.88 = f32[2048,768]{0,1} fusion(bf16[1536,768]{0,1:T(8,128)(2,1)} %bitcast.78, bf16[1536,2048]{1,0:T(8,128)(2,1)} %param.13, f32[2048]{0:T(1024)S(1)} %copy-done.8, f32[1536]{0:T(1024)S(1)} %copy-done.12, f32[1536]{0:T(1024)S(1)} %copy-done.14), kind=kOutput, calls=%fused_computation.94 | convolution fusion | flops 4847566848 | bytes 14962688
  319.1 431.5 %all-reduce.8 = (bf16[2048,3,4,64]{0,3,2,1:T(8,128)(2,1)}, bf16[4,64,2048]{2,1,0:T(8,128)(2,1)}, bf16[2048,1024]{1,0:T(8,128)(2,1)}, bf16[1024,2048]{1,0:T(8,128)(2,1)}) all-reduce(f32[2048,3,4,64]{0,3,2,1:T(8,128)} %bitcast.76, f32[4,64,2048]{2,1,0:T(8,128)} %fusion.34, ...), channel_id=1, replica_groups=mesh['pod'=1,'dp'=4,'tp'=8] {'dp'}, use_global_device_ids=true, to_apply=%region_9.10 | all-reduce | flops 6291456 | bytes 37748736 | tf_op jit(solution)/shard_map/psum | solution.py:83
  750.6 7.7 fusion.17
  758.3 11.8 %add_convert_fusion = bf16[1536,2048]{1,0:T(8,128)(2,1)} fusion(f32[1536,2048]{1,0:T(8,128)} %copy-done.1, bf16[1536,2048]{1,0:T(8,128)(2,1)S(1)} %copy-done.3, bf16[1536,2048]{1,0:T(8,128)(2,1)} %param.13, f32[1536]{0:T(1024)S(1)} %broadcast_multiply_fusion, f32[1536]{0:T(1024)S(1)} %broadcast_multiply_fusion.1, f32[2048]{0:T(1024)S(1)} %copy-done.8, ...), kind=kLoop, calls=%fused_computation.23 | loop fusion | flops 34603008 | bytes 31490048 | tf_op jit(solution)/shard_map/convert_element_type | solution.py:81
  (28 shorter events, 0.1 us)
Async XLA Ops:
  7.2 59.6 %copy-start = (bf16[2048,3,4,64]{0,3,2,1:T(8,128)(2,1)S(1)}, bf16[2048,3,4,64]{0,3,2,1:T(8,128)(2,1)}, u32[]{:S(2)}) copy-start(bf16[2048,3,4,64]{0,3,2,1:T(8,128)(2,1)} %param.22) | copy-start | bytes 9437188
  7.2 112.5 %all-reduce.5.cloned.1.call-start = ((), (), s32[]{:S(2)}) async-start(), calls=%async_computation | async-start | bytes 12582912 | tf_op jit(solution)/shard_map/psum | solution.py:67
  8.1 10.5 %copy-start.5 = (bf16[1536,2048]{1,0:T(8,128)(2,1)S(1)}, bf16[1536,2048]{1,0:T(8,128)(2,1)}, u32[]{:S(2)}) copy-start(bf16[1536,2048]{1,0:T(8,128)(2,1)} %param.21) | copy-start | bytes 18874372
  8.1 10.5 %copy-start.16 = (bf16[1024,2048]{1,0:T(8,128)(2,1)S(1)}, bf16[1024,2048]{1,0:T(8,128)(2,1)}, u32[]{:S(2)}) copy-start(bf16[1024,2048]{1,0:T(8,128)(2,1)} %param.25) | copy-start | bytes 12582916
  18.6 10.7 %copy-start.18 = (bf16[1536,1024]{1,0:T(8,128)(2,1)}, bf16[1536,1024]{1,0:T(8,128)(2,1)S(1)}, u32[]{:S(2)}) copy-start(bf16[1536,1024]{1,0:T(8,128)(2,1)S(1)} %convolution_convert_fusion.1) | copy-start | bytes 9437188
  18.6 12.4 %copy-start.17 = (bf16[2048,1024]{1,0:T(8,128)(2,1)S(1)}, bf16[2048,1024]{1,0:T(8,128)(2,1)}, u32[]{:S(2)}) copy-start(bf16[2048,1024]{1,0:T(8,128)(2,1)} %param.24) | copy-start | bytes 12582916
  29.3 1.7 copy-start.20
  39.6 0.7 copy-start.9
  39.6 0.7 copy-start.10
  39.7 710.9 %all-reduce.7.cloned.1.call-start = ((), (), s32[]{:S(2)}) async-start(), calls=%async_computation.1 | async-start | bytes 12582912 | tf_op jit(solution)/shard_map/psum | solution.py:80
  40.3 13.5 %copy-start.19 = (bf16[1536,1024]{1,0:T(8,128)(2,1)S(1)}, bf16[1536,1024]{1,0:T(8,128)(2,1)}, u32[]{:S(2)}) copy-start(bf16[1536,1024]{1,0:T(8,128)(2,1)} %copy-done.18) | copy-start | bytes 9437188
  53.8 13.0 %copy-start.15 = (bf16[2048]{0:T(1024)(128)(2,1)S(1)}, bf16[2048]{0:T(1024)(128)(2,1)}, u32[]{:S(2)}) copy-start(bf16[2048]{0:T(1024)(128)(2,1)} %param.19) | copy-start | bytes 12292
  53.8 13.0 %copy-start.11 = (f32[1536]{0:T(1024)S(1)}, f32[1536]{0:T(1024)}, u32[]{:S(2)}) copy-start(f32[1536]{0:T(1024)} %param.15) | copy-start | bytes 18436
  53.8 13.0 %copy-start.13 = (f32[1536]{0:T(1024)S(1)}, f32[1536]{0:T(1024)}, u32[]{:S(2)}) copy-start(f32[1536]{0:T(1024)} %param.16) | copy-start | bytes 18436
  66.8 7.6 copy-start.7
  119.7 7.7 copy-start.2
  127.4 12.7 %copy-start.6 = (bf16[4,64,2048]{2,1,0:T(8,128)(2,1)S(1)}, bf16[4,64,2048]{2,1,0:T(8,128)(2,1)}, u32[]{:S(2)}) copy-start(bf16[4,64,2048]{2,1,0:T(8,128)(2,1)} %param.23) | copy-start | bytes 3145732
  135.5 4.5 copy-start.1
  142.0 16.2 %copy-start.4 = (bf16[1536,4,64]{0,2,1:T(8,128)(2,1)}, bf16[1536,4,64]{0,2,1:T(8,128)(2,1)S(1)}, u32[]{:S(2)}) copy-start(bf16[1536,4,64]{0,2,1:T(8,128)(2,1)S(1)} %fusion.58) | copy-start | bytes 2359300
  308.4 0.7 copy-start.8
  308.4 0.7 copy-start.12
  308.4 0.7 copy-start.14
  750.6 7.7 copy-start.3
Sparse Core Ops, SparseCore 0:
  39.8 79.8 all-reduce.4
  308.6 78.9 all-reduce.6
where the time goes:
time: 786 us; the launch traced here: 777 us
  blocking collectives  432 us (55%)
  matrix products  261 us (33%)
  other arithmetic  43.2 us (5%)
  waiting for transfers between devices  19.3 us (2%)
  between operations  14.7 us (2%)
    psum x1, blocking collectives, local_step(): lax.psum(grad_qkv, 'dp').astype(jnp.bfloat16)  432 us
    dot_general x1, matrix products, attn_grads(): jnp.einsum('hqk,qhe->khe', d_scores, qkv_heads[:, 0], preferred_element_t...  49.1 us
    dot_general x1, matrix products, attn_grads(): jnp.einsum('hqk,khe->qhe', d_scores, qkv_heads[:, 1], preferred_element_t...  48.9 us
    sub x1, matrix products, causal_probs(): shifted = jnp.exp(scores - jnp.max(scores, axis=-1, keepdims=True))  22.3 us
    dot_general x1, matrix products, attn_grads(): jnp.einsum('hqk,qhe->khe', prob_lo, d_attn, preferred_element_type=jnp.fl...  20.6 us
    dot_general x1, matrix products, local_step(): jnp.einsum('the,td->hed', attn_out, d_mid_lo, preferred_element_type=jnp....  19.8 us
    psum x1, waiting for transfers between devices, local_step(): d_norm_two = lax.psum(part_two, 'tp').astype(jnp.float32)  19.2 us
    unnamed x2, matrix products  17.5 us
  transfers between devices with their start and end apart: 2, of which 1 were waited for; matrix products, arithmetic and copies ran while one was open for 9% of the time, Pallas kernels for 0%

commit v1 on v0

v1 whole, which is shorter than its diff:
```python
import functools
import math
import jax
import jax.numpy as jnp
from jax import lax
from jax.experimental import pallas as pl
from jax.experimental.pallas import tpu as pltpu
from jax.sharding import PartitionSpec as P

GELU_C = math.sqrt(2.0 / math.pi)
LOG2E = math.log2(math.e)
NT = (((1,), (1,)), ((), ()))
NN = (((1,), (0,)), ((), ()))
TN = (((0,), (0,)), ((), ()))


def dot(lhs, rhs, dims=NN):
    return lax.dot_general(lhs, rhs, dims, preferred_element_type=jnp.float32)


def normed(row_vals, row_mean, row_rstd):
    return (row_vals.astype(jnp.float32) - row_mean[:, None]) * row_rstd[:, None]


def norm_back(d_norm, x_hat, row_rstd, gain_vec):
    scaled = d_norm * gain_vec.astype(jnp.float32)
    scaled_mean = jnp.mean(scaled, axis=-1, keepdims=True)
    proj_mean = jnp.mean(scaled * x_hat, axis=-1, keepdims=True)
    return row_rstd[:, None] * (scaled - scaled_mean - x_hat * proj_mean)


def gelu_pair(pre_act):
    pre_wide = pre_act.astype(jnp.float32)
    tanh_val = jnp.tanh(GELU_C * (pre_wide + 0.044715 * pre_wide * pre_wide * pre_wide))
    gelu_val = 0.5 * pre_wide * (1.0 + tanh_val)
    gelu_slope = 0.5 * (1.0 + tanh_val) + 0.5 * pre_wide * (1.0 - tanh_val * tanh_val) * GELU_C * (1.0 + 0.134145 * pre_wide * pre_wide)
    return gelu_val, gelu_slope


def attn_kernel(head_dim, q_rows, q_ref, k_ref, v_ref, do_ref, o_ref, dqkv_ref, dk_acc, dv_acc):
    toks, lanes = q_ref.shape
    step = pl.program_id(0)
    per_block = lanes // head_dim
    group = step // per_block
    inner = lax.rem(step, per_block)
    width = dqkv_ref.shape[1] // 3
    scale = head_dim ** -0.5

    @pl.when(inner == 0)
    def _():
        dk_acc[...] = jnp.zeros_like(dk_acc)
        dv_acc[...] = jnp.zeros_like(dv_acc)
        o_ref[...] = jnp.zeros_like(o_ref)
        dqkv_ref[:, pl.ds(pl.multiple_of(group * lanes, lanes), lanes)] = jnp.zeros((toks, lanes), dqkv_ref.dtype)

    lane_ids = lax.broadcasted_iota(jnp.int32, (1, lanes), 1)
    mine = lane_ids // head_dim == inner
    zero = jnp.zeros((), jnp.bfloat16)
    k_own = jnp.where(mine, k_ref[...], zero)
    v_own = jnp.where(mine, v_ref[...], zero)
    k_t = k_own.T
    v_t = v_own.T
    q_cols = pl.ds(pl.multiple_of(group * lanes, lanes), lanes)
    for blk in range(toks // q_rows):
        rows = slice(blk * q_rows, (blk + 1) * q_rows)
        keys = (blk + 1) * q_rows
        q_blk = jnp.where(mine, q_ref[rows, :], zero)
        do_blk = jnp.where(mine, do_ref[rows, :], zero)
        s_t = dot(k_own[:keys], q_blk, NT)
        key_ids = lax.broadcasted_iota(jnp.int32, (q_rows, q_rows), 0)
        qry_ids = lax.broadcasted_iota(jnp.int32, (q_rows, q_rows), 1)
        s_diag = jnp.where(key_ids <= qry_ids, s_t[keys - q_rows:], -1e30)
        s_t = s_diag if blk == 0 else jnp.concatenate([s_t[:keys - q_rows], s_diag], axis=0)
        top = jnp.max(s_t, axis=0, keepdims=True)
        e_t = jnp.exp2((s_t - top) * (scale * LOG2E))
        p_t = e_t * (1.0 / jnp.sum(e_t, axis=0, keepdims=True))
        p_lo = p_t.astype(jnp.bfloat16)
        dp_t = dot(v_own[:keys], do_blk, NT)
        dv_acc[:keys] += dot(p_lo, do_blk)
        o_blk = dot(v_t[:, :keys], p_lo)
        o_ref[rows, :] += o_blk.T.astype(o_ref.dtype)
        prod = p_t * dp_t
        row_sum = jnp.sum(prod, axis=0, keepdims=True)
        ds_lo = (prod - p_t * row_sum).astype(jnp.bfloat16)
        dk_acc[:keys] += dot(ds_lo, q_blk)
        dq_blk = dot(k_t[:, :keys], ds_lo) * scale
        dqkv_ref[rows, q_cols] += dq_blk.T.astype(dqkv_ref.dtype)

    @pl.when(inner == per_block - 1)
    def _():
        dqkv_ref[:, pl.ds(pl.multiple_of(width + group * lanes, lanes), lanes)] = (dk_acc[...] * scale).astype(dqkv_ref.dtype)
        dqkv_ref[:, pl.ds(pl.multiple_of(2 * width + group * lanes, lanes), lanes)] = dv_acc[...].astype(dqkv_ref.dtype)


def attention(qkv, d_attn, heads, head_dim, q_rows=256):
    toks, width = d_attn.shape
    lanes = 128
    per_block = lanes // head_dim
    groups = width // lanes
    spec = lambda off: pl.BlockSpec((toks, lanes), lambda h: (0, off * groups + h // per_block))
    pairs = heads * toks * toks // 2
    return pl.pallas_call(
        functools.partial(attn_kernel, head_dim, q_rows),
        grid=(heads,),
        in_specs=[spec(0), spec(1), spec(2), spec(0)],
        out_specs=[spec(0), pl.BlockSpec((toks, 3 * width), lambda h: (0, 0))],
        out_shape=[jax.ShapeDtypeStruct((toks, width), jnp.bfloat16), jax.ShapeDtypeStruct((toks, 3 * width), jnp.bfloat16)],
        scratch_shapes=[pltpu.VMEM((toks, lanes), jnp.float32), pltpu.VMEM((toks, lanes), jnp.float32)],
        compiler_params=pltpu.CompilerParams(dimension_semantics=("arbitrary",), vmem_limit_bytes=48 * 2 ** 20),
        cost_estimate=pl.CostEstimate(flops=6 * 2 * 256 * pairs, bytes_accessed=8 * toks * width * 2, transcendentals=pairs),
        name="attn_fwd_bwd",
    )(qkv, qkv, qkv, d_attn)


def after(first, *later):
    out = lax.optimization_barrier((first,) + later)[1:]
    return out[0] if len(out) == 1 else out


def wide(arr):
    return arr.astype(jnp.float32)


class Ring:
    def __init__(self, axis, ways, lanes):
        self.axis, self.n, self.lanes = axis, ways // lanes, lanes
        self.me = lax.axis_index(axis) // lanes
        hop = lambda d: [(i, ((i // lanes + d) % self.n) * lanes + i % lanes) for i in range(ways)]
        self.right, self.left = hop(1), hop(-1)

    def to(self, arr, pairs):
        return lax.ppermute(arr, self.axis, pairs)

    def at(self, d):
        return lax.rem(self.me + d + self.n, self.n)

    def gather(self, own):
        half = own.shape[0] // 2
        pieces = [(0, 0, own)]
        from_left = from_right = own
        for k in range(1, self.n // 2):
            from_left, from_right = self.to(from_left, self.right), self.to(from_right, self.left)
            pieces += [(-k, 0, from_left), (k, 0, from_right)]
        pieces += [(self.n // 2, 0, self.to(from_left[:half], self.right)), (self.n // 2, half, self.to(from_right[half:], self.left))]
        return pieces

    def placed(self, pieces, rows):
        out = jnp.zeros((self.n * rows,) + pieces[0][2].shape[1:], pieces[0][2].dtype)
        for offset, row, piece in pieces:
            out = lax.dynamic_update_slice_in_dim(out, piece, self.at(offset) * rows + row, 0)
        return out

    def scatter(self, blocks, filler):
        dtype = blocks.dtype
        half = blocks.shape[1] // 2
        blk = lambda d: lax.dynamic_index_in_dim(blocks, self.at(d), 0, keepdims=False)
        far = blk(self.n // 2)
        right, left = self.to(far[:half], self.right), self.to(far[half:], self.left)
        if filler is not None:
            right, left = after(filler, right, left)
        for k in range(self.n // 2 - 1, 0, -1):
            go_right, go_left = blk(k), blk(-k)
            if right.shape[0] == half:
                go_right = jnp.concatenate([(wide(go_right[:half]) + wide(right)).astype(dtype), go_right[half:]], 0)
                go_left = jnp.concatenate([go_left[:half], (wide(go_left[half:]) + wide(left)).astype(dtype)], 0)
            else:
                go_right = (wide(go_right) + wide(right)).astype(dtype)
                go_left = (wide(go_left) + wide(left)).astype(dtype)
            right, left = self.to(go_right, self.right), self.to(go_left, self.left)
        return wide(blk(0)) + wide(right) + wide(left)


def solution(mesh):
    row_spec = P(('pod', 'dp'), None)
    stat_spec = P(('pod', 'dp'))
    in_specs = (row_spec, row_spec, stat_spec, stat_spec, stat_spec, stat_spec, P(None), P(None), row_spec,
                P(None, None, 'tp', None), P('tp', None, None), P(None, 'tp'), P('tp', None))
    out_specs = (row_spec, P('pod', None, 'tp', None), P(('pod', 'tp'), None, None), P('pod', 'tp'), P(('pod', 'tp'), None))
    tp_ways, dp_ways = mesh.shape['tp'], mesh.shape['dp']
    cores = 2

    def local_step(x_saved, h_saved, mean_one, rstd_one, mean_two, rstd_two, gain_one, gain_two, grad_y, w_qkv, w_proj, w_up, w_down):
        toks, dim = x_saved.shape
        _, three, heads, head_dim = w_qkv.shape
        share = toks // tp_ways
        chips = tp_ways // cores
        tp_at = lax.axis_index('tp')
        start = tp_at * share
        cut = lambda arr: lax.dynamic_slice_in_dim(arr, start, share, 0)
        w_qkv_flat = w_qkv.reshape(dim, three * heads * head_dim)
        w_proj_flat = w_proj.reshape(heads * head_dim, dim)
        lo = jnp.bfloat16
        dp_ring = Ring('dp', dp_ways, 1)
        tp_ring = Ring('tp', tp_ways, cores)
        core = lax.rem(tp_at, cores)
        sibling = [(i, i ^ 1) for i in range(tp_ways)]

        def tp_scatter(part, first, second):
            by_core = part.reshape(chips, cores, share, dim)
            mine = lax.dynamic_index_in_dim(by_core, core, 1, keepdims=False)
            other = lax.dynamic_index_in_dim(by_core, 1 - core, 1, keepdims=False)
            other = after(first, lax.ppermute(other, 'tp', sibling))
            pair = (wide(mine) + wide(other)).astype(part.dtype)
            return tp_ring.scatter(pair, second)

        def tp_gather(own, out, first=None):
            for offset, row, piece in tp_ring.gather(own):
                if offset != 0 and first is not None:
                    piece = after(first, piece)
                base = tp_ring.at(offset) * cores
                other = lax.ppermute(piece, 'tp', sibling)
                out = lax.dynamic_update_slice_in_dim(out, piece, (base + core) * share + row, 0)
                out = lax.dynamic_update_slice_in_dim(out, other, (base + 1 - core) * share + row, 0)
            return out

        def dp_scatter(part):
            return lax.psum_scatter(part, 'dp', scatter_dimension=0, tiled=True)

        norm_two = (normed(h_saved, mean_two, rstd_two) * wide(gain_two)).astype(lo)
        pre_act = dot(norm_two, w_up).astype(lo)
        act_out = gelu_pair(pre_act)[0].astype(lo)
        part_down = dot(act_out, grad_y, TN)
        own_down = dp_scatter(part_down)
        pre_act, dy = after(part_down, pre_act, grad_y)
        d_pre = (dot(dy, w_down, NT) * gelu_pair(pre_act)[1]).astype(lo)
        part_two = dot(d_pre, w_up, NT).astype(lo)
        part_up = dot(norm_two, after(part_two, d_pre), TN)
        own_up = dp_scatter(part_up)

        x_in = after(part_up, x_saved)
        norm_one = (normed(x_in, mean_one, rstd_one) * wide(gain_one)).astype(lo)
        qkv = dot(norm_one, w_qkv_flat).astype(lo)
        d_norm_two = tp_scatter(part_two, part_up, qkv)
        hat_cut = normed(cut(h_saved), cut(mean_two), cut(rstd_two))
        d_mid = wide(cut(grad_y)) + norm_back(d_norm_two, hat_cut, cut(rstd_two), gain_two)
        d_mid_cut = d_mid.astype(lo)
        d_mid_lo = tp_gather(d_mid_cut, part_two)
        d_attn = dot(d_mid_lo, w_proj_flat, NT).astype(lo)
        own_down = after(d_attn, own_down).astype(lo)
        down_pieces = dp_ring.gather(own_down)
        attn_out, d_qkv = attention(qkv, after(own_down, d_attn), heads, head_dim)
        part_qkv = dot(norm_one, d_qkv, TN)
        own_qkv = dp_scatter(part_qkv)
        part_one = dot(after(part_qkv, d_qkv), w_qkv_flat, NT).astype(lo)
        part_proj = dot(after(part_one, attn_out), d_mid_lo, TN)
        own_proj = dp_scatter(part_proj)
        own_up = after(part_proj, own_up).astype(lo)
        up_pieces = dp_ring.gather(own_up)
        d_norm_one = tp_scatter(part_one, own_up, None)
        x_hat_cut = normed(cut(x_saved), cut(mean_one), cut(rstd_one))
        grad_x_cut = (d_mid + norm_back(d_norm_one, x_hat_cut, cut(rstd_one), gain_one)).astype(lo)
        own_qkv = own_qkv.astype(lo)
        grad_x = tp_gather(grad_x_cut, part_one, own_qkv)

        qkv_pieces = dp_ring.gather(own_qkv)
        late = lambda first, pieces: [(at, row, after(first, piece)) for at, row, piece in pieces]
        up_pieces = up_pieces[:-2] + late(own_qkv, up_pieces[-2:])
        own_proj = after((grad_x, qkv_pieces[:-2]), own_proj).astype(lo)
        proj_pieces = dp_ring.gather(own_proj)
        grad_down = dp_ring.placed(down_pieces, own_down.shape[0])
        grad_up = dp_ring.placed(up_pieces, own_up.shape[0])
        grad_qkv = dp_ring.placed(qkv_pieces, own_qkv.shape[0])
        grad_proj = dp_ring.placed(proj_pieces, own_proj.shape[0])
        return (grad_x, grad_qkv.reshape(w_qkv.shape), grad_proj.reshape(w_proj.shape), grad_up, grad_down)

    return jax.shard_map(local_step, mesh=mesh, in_specs=in_specs, out_specs=out_specs, check_vma=False)
```

time: 786 us -> 446 us (0.57)
  blocking collectives: 432 us -> 0 us
  matrix products: 261 us -> 91.3 us
  waiting for transfers between devices: 19.3 us -> 134 us
  local copies, waits for them, and re-layouts: 7.31 us -> 94.3 us
  starting transfers between devices: 0.34 us -> 43.1 us
  Pallas kernels: 0 us -> 27 us
  other arithmetic: 43.2 us -> 34.8 us
    psum x1 -> x0, blocking collectives: 432 us -> none  [local_step(): lax.psum(grad_qkv, 'dp').astype(jnp.bfloat16)]
    ppermute x0 -> x44, waiting for transfers between devices: none -> 134 us  [the longest x32 128 us: to(): return lax.ppermute(arr, self.axis, pairs)]
    dot_general x12 -> x10, matrix products: 221 us -> 91.3 us  [dot(): return lax.dot_general(lhs, rhs, dims, preferred_element_type=jnp.float32)]
    dynamic_update_slice x0 -> x35, local copies, waits for them, and re-layouts: none -> 49.7 us  [the longest x17 25.1 us: placed(): lax.dynamic_update_slice_in_dim(out, piece, self.at(offset) * rows + row, 0)]
    ppermute x0 -> x44, starting transfers between devices: none -> 42.5 us  [the longest x32 41.3 us: to(): return lax.ppermute(arr, self.axis, pairs)]
    pallas_call x0 -> x1, Pallas kernels: none -> 27 us  [attention(): pl.pallas_call(functools.partial(attn_kernel, head_dim, q_rows), grid=(he...]
    sub x1 -> x0, matrix products: 22.3 us -> none  [causal_probs(): shifted = jnp.exp(scores - jnp.max(scores, axis=-1, keepdims=True))]
    psum x2 -> x0, waiting for transfers between devices: 19.2 us -> none  [the longest x1 19.2 us: local_step(): d_norm_two = lax.psum(part_two, 'tp').astype(jnp.float32)]
  transfers between devices with their start and end apart: 2 -> 48, of which waited for: 1 -> 16; matrix products, arithmetic and copies ran while one was open for 9% -> 43% of each run, Pallas kernels for 0% -> 6%
where the time goes in v1:
time: 446 us; the launch traced here: 439 us
  waiting for transfers between devices  134 us (30%)
  local copies, waits for them, and re-layouts  94.3 us (21%)
  matrix products  91.3 us (20%)
  starting transfers between devices  43.1 us (10%)
  other arithmetic  34.8 us (8%)
  Pallas kernels  27 us (6%)
  between operations  14.5 us (3%)
    ppermute x32, waiting for transfers between devices, to(): return lax.ppermute(arr, self.axis, pairs)  128 us
    dot_general x10, matrix products, dot(): return lax.dot_general(lhs, rhs, dims, preferred_element_type=jnp.float32)  91.3 us
    ppermute x32, starting transfers between devices, to(): return lax.ppermute(arr, self.axis, pairs)  41.3 us
    pallas_call x1, Pallas kernels, attention(): pl.pallas_call(functools.partial(attn_kernel, head_dim, q_rows), grid=(he...  27 us
    dynamic_update_slice x17, local copies, waits for them, and re-layouts, placed(): lax.dynamic_update_slice_in_dim(out, piece, self.at(offset) * rows + row, 0)  25.1 us
    dynamic_update_slice x10, local copies, waits for them, and re-layouts, tp_gather(): lax.dynamic_update_slice_in_dim(out, other, (base + 1 - core) * share + r...  13.4 us
    dynamic_update_slice x8, local copies, waits for them, and re-layouts, tp_gather(): lax.dynamic_update_slice_in_dim(out, piece, (base + core) * share + row, 0)  11.2 us
  transfers between devices with their start and end apart: 48, of which 16 were waited for; matrix products, arithmetic and copies ran while one was open for 43% of the time, Pallas kernels for 6%

profile of v1, /device:TPU:102, one launch (start us, length us, event | category | flops | bytes accessed | tf_op | source)
XLA Modules:
  0.0 439.0 jit_solution(10123027452917821043)
XLA Ops:
  8.1 10.5 %convolution_convert_fusion.2 = bf16[1536,1024]{1,0:T(8,128)(2,1)S(1)} fusion(bf16[2048,1024]{1,0:T(8,128)(2,1)} %param.24, bf16[1536,2048]{1,0:T(8,128)(2,1)} %param.14, f32[2048]{0:T(1024)S(1)} %convert_element_type.171, f32[1536]{0:T(1024)} %param.18, f32[1536]{0:T(1024)} %param.17), kind=kOutput, calls=%fused_computation.34 | convolution fusion | flops 6459752448 | bytes 13651968 | tf_op jit(solution)/shard_map/dot_general | solution.py:18
  20.3 10.0 %fusion.16 = f32[1024,2048]{1,0:T(8,128)} fusion(bf16[1536,2048]{1,0:T(8,128)(2,1)S(1)} %copy-done.16, bf16[1536,1024]{1,0:T(8,128)(2,1)S(1)} %convolution_convert_fusion.2), kind=kOutput, calls=%fused_computation.36 | convolution fusion | flops 6458179584 | bytes 17825792 | tf_op jit(solution)/shard_map/dot_general | solution.py:18
  30.6 13.8 %fusion.12 = bf16[1536,1024]{1,0:T(8,128)(2,1)S(1)} fusion(bf16[1536,1024]{1,0:T(8,128)(2,1)} %copy-done.24, bf16[1536,2048]{1,0:T(8,128)(2,1)} %param.21, bf16[1024,2048]{1,0:T(8,128)(2,1)} %param.25), kind=kOutput, calls=%fused_computation.28 | convolution fusion | flops 6473908224 | bytes 16777216 | tf_op jit(solution)/shard_map/dot_general | solution.py:18
  44.4 8.7 %convolution_convert_fusion.1 = bf16[1536,2048]{1,0:T(8,128)(2,1)} fusion(bf16[1536,1024]{1,0:T(8,128)(2,1)S(1)} %fusion.12, bf16[2048,1024]{1,0:T(8,128)(2,1)S(1)} %copy-done.22), kind=kOutput, calls=%fused_computation.15 | convolution fusion | flops 6445596672 | bytes 13631488 | tf_op jit(solution)/shard_map/dot_general | solution.py:18
  53.1 11.4 %fusion.36 = f32[2048,1024]{1,0:T(8,128)} fusion(bf16[1536,1024]{1,0:T(8,128)(2,1)S(1)} %fusion.12, bf16[1536,2048]{1,0:T(8,128)(2,1)} %param.14, f32[2048]{0:T(1024)S(1)} %convert_element_type.171, f32[1536]{0:T(1024)S(1)} %copy-done.18, f32[1536]{0:T(1024)S(1)} %copy-done.19), kind=kOutput, calls=%fused_computation.130 | convolution fusion | flops 6458179584 | bytes 17846272 | tf_op jit(solution)/shard_map/dot_general | solution.py:18
  64.9 4.0 dynamic-slice_bitcast_fusion.1
  68.9 5.9 %collective-permute-done = bf16[4,192,2048]{2,1,0:T(8,128)(2,1)} collective-permute-done((bf16[4,192,2048]{2,1,0:T(8,128)(2,1)}, bf16[4,192,2048]{2,1,0:T(8,128)(2,1)}, u32[]{:S(2)}, u32[]{:S(2)}) %collective-permute-start) | collective-permute-done | bytes 3145760 | tf_op jit(solution)/shard_map/ppermute | solution.py:202
  74.9 4.2 fusion.15
  81.4 8.7 %convolution_convert_fusion.3.q_ref.k_ref.v_ref = bf16[1536,768]{1,0:T(8,128)(2,1)} fusion(bf16[2048,768]{0,1:T(8,128)(2,1)S(1)} %bitcast.91, bf16[1536,2048]{1,0:T(8,128)(2,1)} %param.13, f32[2048]{0:T(1024)S(1)} %convert_element_type.180, f32[1536]{0:T(1024)S(1)} %copy-done.20, f32[1536]{0:T(1024)S(1)} %copy-done.21), kind=kOutput, calls=%fused_computation.35 | convolution fusion | flops 4848746496 | bytes 11816960 | tf_op jit(solution)/shard_map/dot_general | solution.py:18
  96.7 16.0 %collective-permute-done.3 = bf16[192,2048]{1,0:T(8,128)(2,1)} collective-permute-done((bf16[192,2048]{1,0:T(8,128)(2,1)}, bf16[192,2048]{1,0:T(8,128)(2,1)}, u32[]{:S(2)}, u32[]{:S(2)}) %collective-permute-start.3) | collective-permute-done | bytes 786464 | tf_op jit(solution)/shard_map/ppermute | solution.py:132
  112.7 2.4 collective-permute-done.4
  115.1 2.6 fusion.30
  117.7 5.0 %constant_dynamic-update-slice_fusion.39 = (bf16[1536,2048]{1,0:T(8,128)(2,1)}, bf16[192,2048]{1,0:T(8,128)(2,1)}, f32[192,2048]{1,0:T(8,128)}) fusion(bf16[1536,2048]{1,0:T(8,128)(2,1)} %convolution_convert_fusion.1, s32[]{:T(128)S(6)} %select_n.141, f32[192]{0:T(256)S(1)} %get-tuple-element.76, f32[192]{0:T(256)S(1)} %dynamic_slice.70, ...), kind=kLoop, calls=%fused_computation.121 | loop fusion | flops 6291456 | bytes 7089164 | tf_op jit(solution)/shard_map/dynamic_update_slice | solution.py:212
  124.7 15.9 %collective-permute-done.6 = bf16[192,2048]{1,0:T(8,128)(2,1)} collective-permute-done((bf16[192,2048]{1,0:T(8,128)(2,1)}, bf16[192,2048]{1,0:T(8,128)(2,1)}, u32[]{:S(2)}, u32[]{:S(2)}) %collective-permute-start.6) | collective-permute-done | bytes 786464 | tf_op jit(solution)/shard_map/ppermute | solution.py:132
  149.1 4.2 collective-permute-done.10
  153.3 3.5 collective-permute-done.12
  156.8 2.1 constant_dynamic-update-slice_fusion.36
  165.2 5.6 %convolution_convert_fusion.4.do_ref = bf16[1536,256]{1,0:T(8,128)(2,1)} fusion(bf16[1536,2048]{1,0:T(8,128)(2,1)} %constant_dynamic-update-slice_fusion.30, bf16[256,2048]{1,0:T(8,128)(2,1)S(1)} %bitcast.98), kind=kOutput, calls=%fused_computation.43 | convolution fusion | flops 1611005952 | bytes 8126464 | tf_op jit(solution)/shard_map/dot_general | solution.py:18
  170.8 2.7 broadcast_in_dim.11
  175.1 27.0 %attn_fwd_bwd.1 = (bf16[1536,256]{1,0:T(8,128)(2,1)S(1)}, bf16[1536,768]{1,0:T(8,128)(2,1)S(1)}) custom-call(bf16[1536,768]{1,0:T(8,128)(2,1)} %convolution_convert_fusion.3.q_ref.k_ref.v_ref, bf16[1536,768]{1,0:T(8,128)(2,1)} %convolution_convert_fusion.3.q_ref.k_ref.v_ref, bf16[1536,768]{1,0:T(8,128)(2,1)} %convolution_convert_fusion.3.q_ref.k_ref.v_ref, ...), custom_call_target="tpu_custom_call" | custom-call | flops 14495514624 | bytes 6291456 | tf_op jit(solution)/shard_map/attn_fwd_bwd/pallas_call | solution.py:102
  204.4 7.7 %fusion.37 = f32[2048,768]{1,0:T(8,128)} fusion(bf16[1536,768]{1,0:T(8,128)(2,1)S(1)} %get-tuple-element.37, bf16[1536,2048]{1,0:T(8,128)(2,1)S(1)} %bitcast.97, f32[2048]{0:T(1024)S(1)} %convert_element_type.180, f32[1536]{0:T(1024)S(1)} %copy-done.20, f32[1536]{0:T(1024)S(1)} %copy-done.21), kind=kOutput, calls=%fused_computation.131 | convolution fusion | flops 4847566848 | bytes 14962688 | tf_op jit(solution)/shard_map/dot_general | solution.py:18
  212.3 8.8 %convolution_convert_fusion = bf16[1536,2048]{1,0:T(8,128)(2,1)} fusion(bf16[1536,768]{1,0:T(8,128)(2,1)} %copy-done.3, bf16[2048,768]{0,1:T(8,128)(2,1)S(1)} %bitcast.92), kind=kOutput, calls=%fused_computation.14 | convolution fusion | flops 4834983936 | bytes 11796480 | tf_op jit(solution)/shard_map/dot_general | solution.py:18
  221.1 4.6 %dynamic-slice_bitcast_fusion = bf16[4,192,2048]{2,1,0:T(8,128)(2,1)} fusion(bf16[4,2,192,2048]{3,2,1,0:T(8,128)(2,1)} %bitcast.12, s32[]{:T(128)S(6)} %select_n.135), kind=kLoop, calls=%fused_computation.37 | loop fusion | bytes 6291460 | tf_op jit(solution)/shard_map/jit(dynamic_index_in_dim)/squeeze | solution.py:201
  226.2 6.2 %fusion.38 = f32[256,2048]{1,0:T(8,128)} fusion(bf16[1536,256]{1,0:T(8,128)(2,1)} %copy-done.1, bf16[1536,2048]{1,0:T(8,128)(2,1)} %constant_dynamic-update-slice_fusion.30), kind=kOutput, calls=%fused_computation.132 | convolution fusion | flops 1610612736 | bytes 9175040 | tf_op jit(solution)/shard_map/dot_general | solution.py:18
  232.3 2.5 broadcast_in_dim.10
  236.5 4.3 fusion.14
  244.3 2.6 collective-permute-start.41
  246.9 5.2 %collective-permute-done.15 = bf16[96,2048]{1,0:T(8,128)(2,1)S(1)} collective-permute-done((bf16[96,2048]{1,0:T(8,128)(2,1)S(1)}, bf16[96,2048]{1,0:T(8,128)(2,1)S(1)}, u32[]{:S(2)}, u32[]{:S(2)}) %collective-permute-start.15) | collective-permute-done | bytes 393248 | tf_op jit(solution)/shard_map/ppermute | solution.py:132
  257.9 35.8 %collective-permute-done.40 = bf16[256,2048]{1,0:T(8,128)(2,1)} collective-permute-done((bf16[256,2048]{1,0:T(8,128)(2,1)}, bf16[256,2048]{1,0:T(8,128)(2,1)}, u32[]{:S(2)}, u32[]{:S(2)}) %collective-permute-start.40) | collective-permute-done | bytes 1048608 | tf_op jit(solution)/shard_map/ppermute | solution.py:132
  298.1 27.6 %collective-permute-done.36 = bf16[512,1024]{1,0:T(8,128)(2,1)} collective-permute-done((bf16[512,1024]{1,0:T(8,128)(2,1)}, bf16[512,1024]{1,0:T(8,128)(2,1)}, u32[]{:S(2)}, u32[]{:S(2)}) %collective-permute-start.36) | collective-permute-done | bytes 1048608 | tf_op jit(solution)/shard_map/ppermute | solution.py:132
  326.7 2.3 constant_dynamic-update-slice_fusion.8
  329.0 2.3 constant_dynamic-update-slice_fusion.3
  331.3 2.4 fusion.31
  333.7 3.7 constant_dynamic-update-slice_fusion.29
  338.0 2.6 collective-permute-start.20
  344.4 2.3 constant_dynamic-update-slice_fusion.2
  351.4 4.9 %collective-permute-done.22 = bf16[192,2048]{1,0:T(8,128)(2,1)S(1)} collective-permute-done((bf16[192,2048]{1,0:T(8,128)(2,1)}, bf16[192,2048]{1,0:T(8,128)(2,1)S(1)}, u32[]{:S(2)}, u32[]{:S(2)}) %collective-permute-start.22) | collective-permute-done | bytes 786464 | tf_op jit(solution)/shard_map/ppermute | solution.py:132
  358.9 3.2 collective-permute-start.24
  362.1 2.4 convert_element_type.224
  366.6 2.3 copy.25
  373.2 2.3 constant_dynamic-update-slice_fusion.5
  387.8 2.9 collective-permute-done.28
  390.7 4.8 %collective-permute-done.29 = bf16[512,768]{1,0:T(8,128)(2,1)} collective-permute-done((bf16[512,768]{1,0:T(8,128)(2,1)}, bf16[512,768]{1,0:T(8,128)(2,1)}, u32[]{:S(2)}, u32[]{:S(2)}) %collective-permute-start.29) | collective-permute-done | bytes 786464 | tf_op jit(solution)/shard_map/ppermute | solution.py:132
  398.6 3.1 collective-permute-start.33
  405.2 3.2 collective-permute-start.31
  408.5 2.3 copy.26
  410.8 2.4 copy.27
  419.5 3.2 collective-permute-start.35
  (203 shorter events, 102.6 us)
Async XLA Ops:
  7.2 163.6 %reduce-scatter.5.cloned.1.call-start = ((), (), s32[]{:S(2)}) async-start(), calls=%async_computation.4 | async-start | bytes 10485760 | tf_op jit(solution)/shard_map/reduce_scatter | solution.py:217
  30.3 202.0 %reduce-scatter.7.cloned.1.call-start = ((), (), s32[]{:S(2)}) async-start(), calls=%async_computation.5 | async-start | bytes 10485760 | tf_op jit(solution)/shard_map/reduce_scatter | solution.py:217
  64.6 297.5 %reduce-scatter.9.cloned.1.call-start = ((), (), s32[]{:S(2)}) async-start(), calls=%async_computation.6 | async-start | bytes 7864320 | tf_op jit(solution)/shard_map/reduce_scatter | solution.py:217
  68.9 6.0 %collective-permute-start = (bf16[4,192,2048]{2,1,0:T(8,128)(2,1)}, bf16[4,192,2048]{2,1,0:T(8,128)(2,1)}, u32[]{:S(2)}, u32[]{:S(2)}) collective-permute-start(bf16[4,192,2048]{2,1,0:T(8,128)(2,1)} %dynamic-slice_bitcast_fusion.1), channel_id=1, source_target_pairs={{0,1},{1,0},{2,3},{3,2},{4,5},{5,4},{6,7},{7,6},{8,9},{9,8},{10,11... | collective-permute-start | bytes 9437192 | tf_op jit(solution)/shard_map/ppermute | solution.py:202
  79.3 11.4 %collective-permute-start.1 = (bf16[96,2048]{1,0:T(8,128)(2,1)S(1)}, bf16[96,2048]{1,0:T(8,128)(2,1)S(1)}, u32[]{:S(2)}, u32[]{:S(2)}) collective-permute-start(bf16[96,2048]{1,0:T(8,128)(2,1)S(1)} %get-tuple-element.74), channel_id=1, source_target_pairs={{0,2},{1,3},{2,4},{3,5},{4,6},{5,7},{6,0},{7,1},{8,10},{9,11},{10,... | collective-permute-start | bytes 1179656 | tf_op jit(solution)/shard_map/ppermute | solution.py:132
  80.0 12.3 %collective-permute-start.2 = (bf16[96,2048]{1,0:T(8,128)(2,1)S(1)}, bf16[96,2048]{1,0:T(8,128)(2,1)S(1)}, u32[]{:S(2)}, u32[]{:S(2)}) collective-permute-start(bf16[96,2048]{1,0:T(8,128)(2,1)S(1)} %get-tuple-element.75), channel_id=1, source_target_pairs={{0,6},{1,7},{2,0},{3,1},{4,2},{5,3},{6,4},{7,5},{8,14},{9,15},{10,... | collective-permute-start | bytes 1179656 | tf_op jit(solution)/shard_map/ppermute | solution.py:132
  93.6 19.1 %collective-permute-start.3 = (bf16[192,2048]{1,0:T(8,128)(2,1)}, bf16[192,2048]{1,0:T(8,128)(2,1)}, u32[]{:S(2)}, u32[]{:S(2)}) collective-permute-start(bf16[192,2048]{1,0:T(8,128)(2,1)} %pad_maximum_fusion), channel_id=1, source_target_pairs={{0,2},{1,3},{2,4},{3,5},{4,6},{5,7},{6,0},{7,1},{8,10},{9,11},{10,... | collective-permute-start | bytes 2359304 | tf_op jit(solution)/shard_map/ppermute | solution.py:132
  94.8 20.3 %collective-permute-start.4 = (bf16[192,2048]{1,0:T(8,128)(2,1)}, bf16[192,2048]{1,0:T(8,128)(2,1)}, u32[]{:S(2)}, u32[]{:S(2)}) collective-permute-start(bf16[192,2048]{1,0:T(8,128)(2,1)} %pad_maximum_fusion.1), channel_id=1, source_target_pairs={{0,6},{1,7},{2,0},{3,1},{4,2},{5,3},{6,4},{7,5},{8,14},{9,15},{10,... | collective-permute-start | bytes 2359304 | tf_op jit(solution)/shard_map/ppermute | solution.py:132
  122.7 17.9 %collective-permute-start.6 = (bf16[192,2048]{1,0:T(8,128)(2,1)}, bf16[192,2048]{1,0:T(8,128)(2,1)}, u32[]{:S(2)}, u32[]{:S(2)}) collective-permute-start(bf16[192,2048]{1,0:T(8,128)(2,1)} %get-tuple-element.62), channel_id=1, source_target_pairs={{0,2},{1,3},{2,4},{3,5},{4,6},{5,7},{6,0},{7,1},{8,10},{9,11},{10,... | collective-permute-start | bytes 2359304 | tf_op jit(solution)/shard_map/ppermute | solution.py:132
  122.7 20.5 %collective-permute-start.8 = (bf16[192,2048]{1,0:T(8,128)(2,1)}, bf16[192,2048]{1,0:T(8,128)(2,1)}, u32[]{:S(2)}, u32[]{:S(2)}) collective-permute-start(bf16[192,2048]{1,0:T(8,128)(2,1)} %get-tuple-element.62), channel_id=1, source_target_pairs={{0,6},{1,7},{2,0},{3,1},{4,2},{5,3},{6,4},{7,5},{8,14},{9,15},{10,... | collective-permute-start | bytes 2359304 | tf_op jit(solution)/shard_map/ppermute | solution.py:132
  124.7 20.2 %collective-permute-start.5 = (bf16[192,2048]{1,0:T(8,128)(2,1)}, bf16[192,2048]{1,0:T(8,128)(2,1)}, u32[]{:S(2)}, u32[]{:S(2)}) collective-permute-start(bf16[192,2048]{1,0:T(8,128)(2,1)} %get-tuple-element.62), channel_id=1, source_target_pairs={{0,1},{1,0},{2,3},{3,2},{4,5},{5,4},{6,7},{7,6},{8,9},{9,8},{10,11... | collective-permute-start | bytes 2359304 | tf_op jit(solution)/shard_map/ppermute | solution.py:211
  140.6 16.2 %collective-permute-start.7 = (bf16[192,2048]{1,0:T(8,128)(2,1)}, bf16[192,2048]{1,0:T(8,128)(2,1)}, u32[]{:S(2)}, u32[]{:S(2)}) collective-permute-start(bf16[192,2048]{1,0:T(8,128)(2,1)} %collective-permute-done.6), channel_id=1, source_target_pairs={{0,1},{1,0},{2,3},{3,2},{4,5},{5,4},{6,7},{7,6},{8,9},{9,8},{10,11... | collective-permute-start | bytes 2359304 | tf_op jit(solution)/shard_map/ppermute | solution.py:211
  141.7 11.6 %collective-permute-start.10 = (bf16[96,2048]{1,0:T(8,128)(2,1)S(1)}, bf16[96,2048]{1,0:T(8,128)(2,1)S(1)}, u32[]{:S(2)}, u32[]{:S(2)}) collective-permute-start(bf16[96,2048]{1,0:T(8,128)(2,1)S(1)} %slice.132), channel_id=1, source_target_pairs={{0,2},{1,3},{2,4},{3,5},{4,6},{5,7},{6,0},{7,1},{8,10},{9,11},{10,... | collective-permute-start | bytes 1179656 | tf_op jit(solution)/shard_map/ppermute | solution.py:132
  144.3 12.5 %collective-permute-start.12 = (bf16[96,2048]{1,0:T(8,128)(2,1)S(1)}, bf16[96,2048]{1,0:T(8,128)(2,1)S(1)}, u32[]{:S(2)}, u32[]{:S(2)}) collective-permute-start(bf16[96,2048]{1,0:T(8,128)(2,1)S(1)} %slice.133), channel_id=1, source_target_pairs={{0,6},{1,7},{2,0},{3,1},{4,2},{5,3},{6,4},{7,5},{8,14},{9,15},{10,... | collective-permute-start | bytes 1179656 | tf_op jit(solution)/shard_map/ppermute | solution.py:132
  144.9 16.1 %collective-permute-start.9 = (bf16[192,2048]{1,0:T(8,128)(2,1)}, bf16[192,2048]{1,0:T(8,128)(2,1)S(1)}, u32[]{:S(2)}, u32[]{:S(2)}) collective-permute-start(bf16[192,2048]{1,0:T(8,128)(2,1)} %collective-permute-done.8), channel_id=1, source_target_pairs={{0,1},{1,0},{2,3},{3,2},{4,5},{5,4},{6,7},{7,6},{8,9},{9,8},{10,11... | collective-permute-start | bytes 2359304 | tf_op jit(solution)/shard_map/ppermute | solution.py:211
  153.3 9.5 %collective-permute-start.11 = (bf16[96,2048]{1,0:T(8,128)(2,1)S(1)}, bf16[96,2048]{1,0:T(8,128)(2,1)S(1)}, u32[]{:S(2)}, u32[]{:S(2)}) collective-permute-start(bf16[96,2048]{1,0:T(8,128)(2,1)S(1)} %collective-permute-done.10), channel_id=1, source_target_pairs={{0,1},{1,0},{2,3},{3,2},{4,5},{5,4},{6,7},{7,6},{8,9},{9,8},{10,11... | collective-permute-start | bytes 1179656 | tf_op jit(solution)/shard_map/ppermute | solution.py:211
  156.8 7.6 %collective-permute-start.13 = (bf16[96,2048]{1,0:T(8,128)(2,1)S(1)}, bf16[96,2048]{1,0:T(8,128)(2,1)S(1)}, u32[]{:S(2)}, u32[]{:S(2)}) collective-permute-start(bf16[96,2048]{1,0:T(8,128)(2,1)S(1)} %collective-permute-done.12), channel_id=1, source_target_pairs={{0,1},{1,0},{2,3},{3,2},{4,5},{5,4},{6,7},{7,6},{8,9},{9,8},{10,11... | collective-permute-start | bytes 1179656 | tf_op jit(solution)/shard_map/ppermute | solution.py:211
  212.2 175.6 %reduce-scatter.11.cloned.1.call-start = ((), (), s32[]{:S(2)}) async-start(), calls=%async_computation.7 | async-start | bytes 2621440 | tf_op jit(solution)/shard_map/reduce_scatter | solution.py:217
  225.7 10.8 %collective-permute-start.14 = (bf16[4,192,2048]{2,1,0:T(8,128)(2,1)}, bf16[4,192,2048]{2,1,0:T(8,128)(2,1)}, u32[]{:S(2)}, u32[]{:S(2)}) collective-permute-start(bf16[4,192,2048]{2,1,0:T(8,128)(2,1)} %dynamic-slice_bitcast_fusion), channel_id=1, source_target_pairs={{0,1},{1,0},{2,3},{3,2},{4,5},{5,4},{6,7},{7,6},{8,9},{9,8},{10,11... | collective-permute-start | bytes 9437192 | tf_op jit(solution)/shard_map/ppermute | solution.py:202
  241.0 11.2 %collective-permute-start.15 = (bf16[96,2048]{1,0:T(8,128)(2,1)S(1)}, bf16[96,2048]{1,0:T(8,128)(2,1)S(1)}, u32[]{:S(2)}, u32[]{:S(2)}) collective-permute-start(bf16[96,2048]{1,0:T(8,128)(2,1)S(1)} %get-tuple-element.66), channel_id=1, source_target_pairs={{0,2},{1,3},{2,4},{3,5},{4,6},{5,7},{6,0},{7,1},{8,10},{9,11},{10,... | collective-permute-start | bytes 1179656 | tf_op jit(solution)/shard_map/ppermute | solution.py:132
  241.1 12.4 %collective-permute-start.17 = (bf16[96,2048]{1,0:T(8,128)(2,1)S(1)}, bf16[96,2048]{1,0:T(8,128)(2,1)S(1)}, u32[]{:S(2)}, u32[]{:S(2)}) collective-permute-start(bf16[96,2048]{1,0:T(8,128)(2,1)S(1)} %get-tuple-element.68), channel_id=1, source_target_pairs={{0,6},{1,7},{2,0},{3,1},{4,2},{5,3},{6,4},{7,5},{8,14},{9,15},{10,... | collective-permute-start | bytes 1179656 | tf_op jit(solution)/shard_map/ppermute | solution.py:132
  243.1 50.6 %collective-permute-start.40 = (bf16[256,2048]{1,0:T(8,128)(2,1)}, bf16[256,2048]{1,0:T(8,128)(2,1)}, u32[]{:S(2)}, u32[]{:S(2)}) collective-permute-start(bf16[256,2048]{1,0:T(8,128)(2,1)} %get-tuple-element.54), channel_id=1, source_target_pairs={{0,8},{8,16},{16,24},{24,0},{1,9},{9,17},{17,25},{25,1},{2,10},{10... | collective-permute-start | bytes 3145736 | tf_op jit(solution)/shard_map/ppermute | solution.py:132
  244.3 52.5 %collective-permute-start.41 = (bf16[256,2048]{1,0:T(8,128)(2,1)}, bf16[256,2048]{1,0:T(8,128)(2,1)}, u32[]{:S(2)}, u32[]{:S(2)}) collective-permute-start(bf16[256,2048]{1,0:T(8,128)(2,1)} %get-tuple-element.54), channel_id=1, source_target_pairs={{0,24},{8,0},{16,8},{24,16},{1,25},{9,1},{17,9},{25,17},{2,26},{10... | collective-permute-start | bytes 3145736 | tf_op jit(solution)/shard_map/ppermute | solution.py:132
  246.9 78.8 %collective-permute-start.36 = (bf16[512,1024]{1,0:T(8,128)(2,1)}, bf16[512,1024]{1,0:T(8,128)(2,1)}, u32[]{:S(2)}, u32[]{:S(2)}) collective-permute-start(bf16[512,1024]{1,0:T(8,128)(2,1)} %get-tuple-element.56), channel_id=1, source_target_pairs={{0,8},{8,16},{16,24},{24,0},{1,9},{9,17},{17,25},{25,1},{2,10},{10... | collective-permute-start | bytes 3145736 | tf_op jit(solution)/shard_map/ppermute | solution.py:132
  254.7 76.6 %collective-permute-start.16 = (bf16[192,2048]{1,0:T(8,128)(2,1)}, bf16[192,2048]{1,0:T(8,128)(2,1)}, u32[]{:S(2)}, u32[]{:S(2)}) collective-permute-start(bf16[192,2048]{1,0:T(8,128)(2,1)} %pad_maximum_fusion.2), channel_id=1, source_target_pairs={{0,2},{1,3},{2,4},{3,5},{4,6},{5,7},{6,0},{7,1},{8,10},{9,11},{10,... | collective-permute-start | bytes 2359304 | tf_op jit(solution)/shard_map/ppermute | solution.py:132
  255.9 75.4 %collective-permute-start.18 = (bf16[192,2048]{1,0:T(8,128)(2,1)}, bf16[192,2048]{1,0:T(8,128)(2,1)}, u32[]{:S(2)}, u32[]{:S(2)}) collective-permute-start(bf16[192,2048]{1,0:T(8,128)(2,1)} %pad_maximum_fusion.3), channel_id=1, source_target_pairs={{0,6},{1,7},{2,0},{3,1},{4,2},{5,3},{6,4},{7,5},{8,14},{9,15},{10,... | collective-permute-start | bytes 2359304 | tf_op jit(solution)/shard_map/ppermute | solution.py:132
  293.7 46.9 %collective-permute-start.37 = (bf16[512,1024]{1,0:T(8,128)(2,1)}, bf16[512,1024]{1,0:T(8,128)(2,1)S(1)}, u32[]{:S(2)}, u32[]{:S(2)}) collective-permute-start(bf16[512,1024]{1,0:T(8,128)(2,1)} %get-tuple-element.56), channel_id=1, source_target_pairs={{0,24},{8,0},{16,8},{24,16},{1,25},{9,1},{17,9},{25,17},{2,26},{10... | collective-permute-start | bytes 3145736 | tf_op jit(solution)/shard_map/ppermute | solution.py:132
  296.8 50.8 %collective-permute-start.42 = (bf16[128,2048]{1,0:T(8,128)(2,1)S(1)}, bf16[128,2048]{1,0:T(8,128)(2,1)S(1)}, u32[]{:S(2)}, u32[]{:S(2)}) collective-permute-start(bf16[128,2048]{1,0:T(8,128)(2,1)S(1)} %slice.142), channel_id=1, source_target_pairs={{0,8},{8,16},{16,24},{24,0},{1,9},{9,17},{17,25},{25,1},{2,10},{10... | collective-permute-start | bytes 1572872 | tf_op jit(solution)/shard_map/ppermute | solution.py:132
  325.7 22.7 %collective-permute-start.43 = (bf16[128,2048]{1,0:T(8,128)(2,1)S(1)}, bf16[128,2048]{1,0:T(8,128)(2,1)S(1)}, u32[]{:S(2)}, u32[]{:S(2)}) collective-permute-start(bf16[128,2048]{1,0:T(8,128)(2,1)S(1)} %slice.143), channel_id=1, source_target_pairs={{0,24},{8,0},{16,8},{24,16},{1,25},{9,1},{17,9},{25,17},{2,26},{10... | collective-permute-start | bytes 1572872 | tf_op jit(solution)/shard_map/ppermute | solution.py:132
  337.4 18.8 %collective-permute-start.22 = (bf16[192,2048]{1,0:T(8,128)(2,1)}, bf16[192,2048]{1,0:T(8,128)(2,1)S(1)}, u32[]{:S(2)}, u32[]{:S(2)}) collective-permute-start(bf16[192,2048]{1,0:T(8,128)(2,1)} %get-tuple-element.60), channel_id=1, source_target_pairs={{0,6},{1,7},{2,0},{3,1},{4,2},{5,3},{6,4},{7,5},{8,14},{9,15},{10,... | collective-permute-start | bytes 2359304 | tf_op jit(solution)/shard_map/ppermute | solution.py:132
  338.0 19.2 %collective-permute-start.20 = (bf16[192,2048]{1,0:T(8,128)(2,1)}, bf16[192,2048]{1,0:T(8,128)(2,1)S(1)}, u32[]{:S(2)}, u32[]{:S(2)}) collective-permute-start(bf16[192,2048]{1,0:T(8,128)(2,1)} %get-tuple-element.60), channel_id=1, source_target_pairs={{0,2},{1,3},{2,4},{3,5},{4,6},{5,7},{6,0},{7,1},{8,10},{9,11},{10,... | collective-permute-start | bytes 2359304 | tf_op jit(solution)/shard_map/ppermute | solution.py:132
  340.6 23.9 %collective-permute-start.19 = (bf16[192,2048]{1,0:T(8,128)(2,1)}, bf16[192,2048]{1,0:T(8,128)(2,1)}, u32[]{:S(2)}, u32[]{:S(2)}) collective-permute-start(bf16[192,2048]{1,0:T(8,128)(2,1)} %get-tuple-element.60), channel_id=1, source_target_pairs={{0,1},{1,0},{2,3},{3,2},{4,5},{5,4},{6,7},{7,6},{8,9},{9,8},{10,11... | collective-permute-start | bytes 2359304 | tf_op jit(solution)/shard_map/ppermute | solution.py:211
  347.6 21.3 %collective-permute-start.39 = (bf16[256,1024]{1,0:T(8,128)(2,1)}, bf16[256,1024]{1,0:T(8,128)(2,1)}, u32[]{:S(2)}, u32[]{:S(2)}) collective-permute-start(bf16[256,1024]{1,0:T(8,128)(2,1)} %slice.141), channel_id=1, source_target_pairs={{0,24},{8,0},{16,8},{24,16},{1,25},{9,1},{17,9},{25,17},{2,26},{10... | collective-permute-start | bytes 1572872 | tf_op jit(solution)/shard_map/ppermute | solution.py:132
  348.5 22.1 %collective-permute-start.38 = (bf16[256,1024]{1,0:T(8,128)(2,1)}, bf16[256,1024]{1,0:T(8,128)(2,1)}, u32[]{:S(2)}, u32[]{:S(2)}) collective-permute-start(bf16[256,1024]{1,0:T(8,128)(2,1)} %slice.140), channel_id=1, source_target_pairs={{0,8},{8,16},{16,24},{24,0},{1,9},{9,17},{17,25},{25,1},{2,10},{10... | collective-permute-start | bytes 1572872 | tf_op jit(solution)/shard_map/ppermute | solution.py:132
  357.1 18.3 %collective-permute-start.26 = (bf16[96,2048]{1,0:T(8,128)(2,1)S(1)}, bf16[96,2048]{1,0:T(8,128)(2,1)}, u32[]{:S(2)}, u32[]{:S(2)}) collective-permute-start(bf16[96,2048]{1,0:T(8,128)(2,1)S(1)} %slice.135), channel_id=1, source_target_pairs={{0,6},{1,7},{2,0},{3,1},{4,2},{5,3},{6,4},{7,5},{8,14},{9,15},{10,... | collective-permute-start | bytes 1179656 | tf_op jit(solution)/shard_map/ppermute | solution.py:132
  358.9 18.4 %collective-permute-start.24 = (bf16[96,2048]{1,0:T(8,128)(2,1)}, bf16[96,2048]{1,0:T(8,128)(2,1)}, u32[]{:S(2)}, u32[]{:S(2)}) collective-permute-start(bf16[96,2048]{1,0:T(8,128)(2,1)} %slice.134), channel_id=1, source_target_pairs={{0,2},{1,3},{2,4},{3,5},{4,6},{5,7},{6,0},{7,1},{8,10},{9,11},{10,... | collective-permute-start | bytes 1179656 | tf_op jit(solution)/shard_map/ppermute | solution.py:132
  364.5 13.8 %collective-permute-start.21 = (bf16[192,2048]{1,0:T(8,128)(2,1)}, bf16[192,2048]{1,0:T(8,128)(2,1)}, u32[]{:S(2)}, u32[]{:S(2)}) collective-permute-start(bf16[192,2048]{1,0:T(8,128)(2,1)} %copy-done.14), channel_id=1, source_target_pairs={{0,1},{1,0},{2,3},{3,2},{4,5},{5,4},{6,7},{7,6},{8,9},{9,8},{10,11... | collective-permute-start | bytes 2359304 | tf_op jit(solution)/shard_map/ppermute | solution.py:211
  368.9 21.8 %collective-permute-start.28 = (bf16[512,768]{1,0:T(8,128)(2,1)}, bf16[512,768]{1,0:T(8,128)(2,1)}, u32[]{:S(2)}, u32[]{:S(2)}) collective-permute-start(bf16[512,768]{1,0:T(8,128)(2,1)} %convert_element_type.224), channel_id=1, source_target_pairs={{0,8},{8,16},{16,24},{24,0},{1,9},{9,17},{17,25},{25,1},{2,10},{10... | collective-permute-start | bytes 2359304 | tf_op jit(solution)/shard_map/ppermute | solution.py:132
  370.6 11.3 %collective-permute-start.23 = (bf16[192,2048]{1,0:T(8,128)(2,1)}, bf16[192,2048]{1,0:T(8,128)(2,1)S(1)}, u32[]{:S(2)}, u32[]{:S(2)}) collective-permute-start(bf16[192,2048]{1,0:T(8,128)(2,1)} %copy-done.12), channel_id=1, source_target_pairs={{0,1},{1,0},{2,3},{3,2},{4,5},{5,4},{6,7},{7,6},{8,9},{9,8},{10,11... | collective-permute-start | bytes 2359304 | tf_op jit(solution)/shard_map/ppermute | solution.py:211
  375.4 20.0 %collective-permute-start.29 = (bf16[512,768]{1,0:T(8,128)(2,1)}, bf16[512,768]{1,0:T(8,128)(2,1)}, u32[]{:S(2)}, u32[]{:S(2)}) collective-permute-start(bf16[512,768]{1,0:T(8,128)(2,1)} %convert_element_type.224), channel_id=1, source_target_pairs={{0,24},{8,0},{16,8},{24,16},{1,25},{9,1},{17,9},{25,17},{2,26},{10... | collective-permute-start | bytes 2359304 | tf_op jit(solution)/shard_map/ppermute | solution.py:132
  377.3 7.2 %collective-permute-start.25 = (bf16[96,2048]{1,0:T(8,128)(2,1)}, bf16[96,2048]{1,0:T(8,128)(2,1)S(1)}, u32[]{:S(2)}, u32[]{:S(2)}) collective-permute-start(bf16[96,2048]{1,0:T(8,128)(2,1)} %collective-permute-done.24), channel_id=1, source_target_pairs={{0,1},{1,0},{2,3},{3,2},{4,5},{5,4},{6,7},{7,6},{8,9},{9,8},{10,11... | collective-permute-start | bytes 1179656 | tf_op jit(solution)/shard_map/ppermute | solution.py:211
  378.3 8.8 %collective-permute-start.27 = (bf16[96,2048]{1,0:T(8,128)(2,1)}, bf16[96,2048]{1,0:T(8,128)(2,1)S(1)}, u32[]{:S(2)}, u32[]{:S(2)}) collective-permute-start(bf16[96,2048]{1,0:T(8,128)(2,1)} %collective-permute-done.26), channel_id=1, source_target_pairs={{0,1},{1,0},{2,3},{3,2},{4,5},{5,4},{6,7},{7,6},{8,9},{9,8},{10,11... | collective-permute-start | bytes 1179656 | tf_op jit(solution)/shard_map/ppermute | solution.py:211
  398.5 18.8 %collective-permute-start.32 = (bf16[64,2048]{1,0:T(8,128)(2,1)}, bf16[64,2048]{1,0:T(8,128)(2,1)S(1)}, u32[]{:S(2)}, u32[]{:S(2)}) collective-permute-start(bf16[64,2048]{1,0:T(8,128)(2,1)} %get-tuple-element.58), channel_id=1, source_target_pairs={{0,8},{8,16},{16,24},{24,0},{1,9},{9,17},{17,25},{25,1},{2,10},{10... | collective-permute-start | bytes 786440 | tf_op jit(solution)/shard_map/ppermute | solution.py:132
  398.6 19.3 %collective-permute-start.33 = (bf16[64,2048]{1,0:T(8,128)(2,1)}, bf16[64,2048]{1,0:T(8,128)(2,1)}, u32[]{:S(2)}, u32[]{:S(2)}) collective-permute-start(bf16[64,2048]{1,0:T(8,128)(2,1)} %get-tuple-element.58), channel_id=1, source_target_pairs={{0,24},{8,0},{16,8},{24,16},{1,25},{9,1},{17,9},{25,17},{2,26},{10... | collective-permute-start | bytes 786440 | tf_op jit(solution)/shard_map/ppermute | solution.py:132
  403.5 21.7 %collective-permute-start.30 = (bf16[256,768]{1,0:T(8,128)(2,1)}, bf16[256,768]{1,0:T(8,128)(2,1)}, u32[]{:S(2)}, u32[]{:S(2)}) collective-permute-start(bf16[256,768]{1,0:T(8,128)(2,1)} %slice.136), channel_id=1, source_target_pairs={{0,8},{8,16},{16,24},{24,0},{1,9},{9,17},{17,25},{25,1},{2,10},{10... | collective-permute-start | bytes 1179656 | tf_op jit(solution)/shard_map/ppermute | solution.py:132
  405.2 23.4 %collective-permute-start.31 = (bf16[256,768]{1,0:T(8,128)(2,1)}, bf16[256,768]{1,0:T(8,128)(2,1)}, u32[]{:S(2)}, u32[]{:S(2)}) collective-permute-start(bf16[256,768]{1,0:T(8,128)(2,1)} %slice.137), channel_id=1, source_target_pairs={{0,24},{8,0},{16,8},{24,16},{1,25},{9,1},{17,9},{25,17},{2,26},{10... | collective-permute-start | bytes 1179656 | tf_op jit(solution)/shard_map/ppermute | solution.py:132
  417.9 8.4 %collective-permute-start.34 = (bf16[32,2048]{1,0:T(8,128)(2,1)}, bf16[32,2048]{1,0:T(8,128)(2,1)}, u32[]{:S(2)}, u32[]{:S(2)}) collective-permute-start(bf16[32,2048]{1,0:T(8,128)(2,1)} %slice.138), channel_id=1, source_target_pairs={{0,8},{8,16},{16,24},{24,0},{1,9},{9,17},{17,25},{25,1},{2,10},{10... | collective-permute-start | bytes 393224 | tf_op jit(solution)/shard_map/ppermute | solution.py:132
  419.5 11.1 %collective-permute-start.35 = (bf16[32,2048]{1,0:T(8,128)(2,1)}, bf16[32,2048]{1,0:T(8,128)(2,1)}, u32[]{:S(2)}, u32[]{:S(2)}) collective-permute-start(bf16[32,2048]{1,0:T(8,128)(2,1)} %slice.139), channel_id=1, source_target_pairs={{0,24},{8,0},{16,8},{24,16},{1,25},{9,1},{17,9},{25,17},{2,26},{10... | collective-permute-start | bytes 393224 | tf_op jit(solution)/shard_map/ppermute | solution.py:132
  (27 other events, 412.8 us)
Sparse Core Ops, SparseCore 0:
  30.4 80.7 reduce-scatter.4
  113.6 77.7 reduce-scatter.6
  212.3 90.9 reduce-scatter.8
  305.5 43.2 reduce-scatter.10

commit v2 on v1

--- a/solution.py
+++ b/solution.py
@@ -121,10 +121,40 @@
     return arr.astype(jnp.float32)
 
 
+def assemble_kernel(places, shape, *refs):
+    n = len(places)
+    pieces, out, held, in_sem, out_sem = refs[:n], refs[n], refs[n + 1:2 * n + 1], refs[2 * n + 1], refs[2 * n + 2]
+    copies_in = [pltpu.make_async_copy(pieces[i], held[i], in_sem.at[i]) for i in range(n)]
+    for copy in copies_in:
+        copy.start()
+    copies_out = []
+    for i, place in enumerate(places):
+        rows = pl.ds(pl.multiple_of(place(), 16), shape[i])
+        copies_in[i].wait()
+        copies_out.append(pltpu.make_async_copy(held[i], out.at[rows], out_sem.at[i]))
+        copies_out[i].start()
+    for copy in copies_out:
+        copy.wait()
+
+
+def assemble(placed):
+    places, pieces = [p for p, _ in placed], [arr for _, arr in placed]
+    n, cols, dtype = len(pieces), pieces[0].shape[1], pieces[0].dtype
+    rows = sum(arr.shape[0] for arr in pieces)
+    return pl.pallas_call(
+        functools.partial(assemble_kernel, places, [arr.shape[0] for arr in pieces]),
+        in_specs=[pl.BlockSpec(memory_space=pl.ANY)] * n,
+        out_specs=pl.BlockSpec(memory_space=pl.ANY),
+        out_shape=jax.ShapeDtypeStruct((rows, cols), dtype),
+        scratch_shapes=[pltpu.VMEM(arr.shape, dtype) for arr in pieces] + [pltpu.SemaphoreType.DMA((n,)), pltpu.SemaphoreType.DMA((n,))],
+        cost_estimate=pl.CostEstimate(flops=1000 * rows * 2, bytes_accessed=4 * rows * cols, transcendentals=0),
+        name="assemble",
+    )(*pieces)
+
+
 class Ring:
     def __init__(self, axis, ways, lanes):
         self.axis, self.n, self.lanes = axis, ways // lanes, lanes
-        self.me = lax.axis_index(axis) // lanes
         hop = lambda d: [(i, ((i // lanes + d) % self.n) * lanes + i % lanes) for i in range(ways)]
         self.right, self.left = hop(1), hop(-1)
 
@@ -132,23 +162,22 @@
         return lax.ppermute(arr, self.axis, pairs)
 
     def at(self, d):
-        return lax.rem(self.me + d + self.n, self.n)
-
-    def gather(self, own):
+        return lax.rem(lax.axis_index(self.axis) // self.lanes + d + self.n, self.n)
+
+    def gather(self, own, way=0):
         half = own.shape[0] // 2
+        far = self.n // 2
         pieces = [(0, 0, own)]
         from_left = from_right = own
-        for k in range(1, self.n // 2):
+        for k in range(1, far):
             from_left, from_right = self.to(from_left, self.right), self.to(from_right, self.left)
             pieces += [(-k, 0, from_left), (k, 0, from_right)]
-        pieces += [(self.n // 2, 0, self.to(from_left[:half], self.right)), (self.n // 2, half, self.to(from_right[half:], self.left))]
-        return pieces
+        if way:
+            return pieces + [(far, 0, self.to(from_left, self.right) if way > 0 else self.to(from_right, self.left))]
+        return pieces + [(far, 0, self.to(from_left[:half], self.right)), (far, half, self.to(from_right[half:], self.left))]
 
     def placed(self, pieces, rows):
-        out = jnp.zeros((self.n * rows,) + pieces[0][2].shape[1:], pieces[0][2].dtype)
-        for offset, row, piece in pieces:
-            out = lax.dynamic_update_slice_in_dim(out, piece, self.at(offset) * rows + row, 0)
-        return out
+        return assemble([(functools.partial(lambda offset, row: self.at(offset) * rows + row, offset, row), arr) for offset, row, arr in pieces])
 
     def scatter(self, blocks, filler):
         dtype = blocks.dtype
@@ -187,7 +216,7 @@
         tp_at = lax.axis_index('tp')
         start = tp_at * share
         cut = lambda arr: lax.dynamic_slice_in_dim(arr, start, share, 0)
-        w_qkv_flat = w_qkv.reshape(dim, three * heads * head_dim)
+        w_qkv_t = w_qkv.transpose(1, 2, 3, 0).reshape(three * heads * head_dim, dim)
         w_proj_flat = w_proj.reshape(heads * head_dim, dim)
         lo = jnp.bfloat16
         dp_ring = Ring('dp', dp_ways, 1)
@@ -203,15 +232,14 @@
             pair = (wide(mine) + wide(other)).astype(part.dtype)
             return tp_ring.scatter(pair, second)
 
-        def tp_gather(own, out, first=None):
+        def tp_gather(own, first=None):
+            placed = []
             for offset, row, piece in tp_ring.gather(own):
                 if offset != 0 and first is not None:
                     piece = after(first, piece)
-                base = tp_ring.at(offset) * cores
-                other = lax.ppermute(piece, 'tp', sibling)
-                out = lax.dynamic_update_slice_in_dim(out, piece, (base + core) * share + row, 0)
-                out = lax.dynamic_update_slice_in_dim(out, other, (base + 1 - core) * share + row, 0)
-            return out
+                at_core = lambda other, offset=offset, row=row: (tp_ring.at(offset) * cores + lax.rem(lax.axis_index('tp') + other, cores)) * share + row
+                placed += [(functools.partial(at_core, 0), piece), (functools.partial(at_core, 1), lax.ppermute(piece, 'tp', sibling))]
+            return assemble(placed)
 
         def dp_scatter(part):
             return lax.psum_scatter(part, 'dp', scatter_dimension=0, tiled=True)
@@ -229,19 +257,19 @@
 
         x_in = after(part_up, x_saved)
         norm_one = (normed(x_in, mean_one, rstd_one) * wide(gain_one)).astype(lo)
-        qkv = dot(norm_one, w_qkv_flat).astype(lo)
+        qkv = dot(norm_one, w_qkv_t, NT).astype(lo)
         d_norm_two = tp_scatter(part_two, part_up, qkv)
         hat_cut = normed(cut(h_saved), cut(mean_two), cut(rstd_two))
         d_mid = wide(cut(grad_y)) + norm_back(d_norm_two, hat_cut, cut(rstd_two), gain_two)
         d_mid_cut = d_mid.astype(lo)
-        d_mid_lo = tp_gather(d_mid_cut, part_two)
+        own_down = after(d_mid_cut, own_down).astype(lo)
+        down_pieces = dp_ring.gather(own_down)
+        d_mid_lo = tp_gather(d_mid_cut, own_down)
         d_attn = dot(d_mid_lo, w_proj_flat, NT).astype(lo)
-        own_down = after(d_attn, own_down).astype(lo)
-        down_pieces = dp_ring.gather(own_down)
-        attn_out, d_qkv = attention(qkv, after(own_down, d_attn), heads, head_dim)
-        part_qkv = dot(norm_one, d_qkv, TN)
+        attn_out, d_qkv = attention(qkv, d_attn, heads, head_dim)
+        part_qkv = dot(d_qkv, norm_one, TN)
         own_qkv = dp_scatter(part_qkv)
-        part_one = dot(after(part_qkv, d_qkv), w_qkv_flat, NT).astype(lo)
+        part_one = dot(after(part_qkv, d_qkv), w_qkv_t).astype(lo)
         part_proj = dot(after(part_one, attn_out), d_mid_lo, TN)
         own_proj = dp_scatter(part_proj)
         own_up = after(part_proj, own_up).astype(lo)
@@ -250,17 +278,17 @@
         x_hat_cut = normed(cut(x_saved), cut(mean_one), cut(rstd_one))
         grad_x_cut = (d_mid + norm_back(d_norm_one, x_hat_cut, cut(rstd_one), gain_one)).astype(lo)
         own_qkv = own_qkv.astype(lo)
-        grad_x = tp_gather(grad_x_cut, part_one, own_qkv)
+        grad_x = tp_gather(grad_x_cut, own_qkv)
 
         qkv_pieces = dp_ring.gather(own_qkv)
         late = lambda first, pieces: [(at, row, after(first, piece)) for at, row, piece in pieces]
         up_pieces = up_pieces[:-2] + late(own_qkv, up_pieces[-2:])
-        own_proj = after((grad_x, qkv_pieces[:-2]), own_proj).astype(lo)
-        proj_pieces = dp_ring.gather(own_proj)
         grad_down = dp_ring.placed(down_pieces, own_down.shape[0])
         grad_up = dp_ring.placed(up_pieces, own_up.shape[0])
+        own_proj = after((grad_x, grad_down, grad_up), own_proj).astype(lo)
+        proj_pieces = dp_ring.gather(own_proj, 1)
         grad_qkv = dp_ring.placed(qkv_pieces, own_qkv.shape[0])
         grad_proj = dp_ring.placed(proj_pieces, own_proj.shape[0])
-        return (grad_x, grad_qkv.reshape(w_qkv.shape), grad_proj.reshape(w_proj.shape), grad_up, grad_down)
+        return (grad_x, grad_qkv.reshape(three, heads, head_dim, dim).transpose(3, 0, 1, 2), grad_proj.reshape(w_proj.shape), grad_up, grad_down)
 
     return jax.shard_map(local_step, mesh=mesh, in_specs=in_specs, out_specs=out_specs, check_vma=False)

time: 446 us -> 424 us (0.951)
  local copies, waits for them, and re-layouts: 94.3 us -> 25.1 us
  waiting for transfers between devices: 134 us -> 160 us
  Pallas kernels: 27 us -> 49.2 us
    dynamic_update_slice x35 -> x0, local copies, waits for them, and re-layouts: 49.7 us -> none  [the longest x17 25.1 us: placed(): lax.dynamic_update_slice_in_dim(out, piece, self.at(offset) * rows + row, 0)]
    ppermute x32 -> x31, waiting for transfers between devices: 128 us -> 153 us  [to(): return lax.ppermute(arr, self.axis, pairs)]
    pallas_call x0 -> x6, Pallas kernels: none -> 22.6 us  [assemble(): pl.pallas_call(functools.partial(assemble_kernel, places, [arr.shape[0] f...]
    convert_element_type x0 -> x5, other arithmetic: none -> 14.8 us  [the longest x1 4.42 us: local_step(): d_mid_cut = d_mid.astype(lo)]
    dynamic_update_slice x5 -> x0, other arithmetic: 13.8 us -> none  [the longest x2 8.68 us: tp_gather(): lax.dynamic_update_slice_in_dim(out, piece, (base + core) * share + row, 0)]
    ppermute x4 -> x0, local copies, waits for them, and re-layouts: 7.01 us -> none  [to(): return lax.ppermute(arr, self.axis, pairs)]
    broadcast_in_dim x4 -> x0, local copies, waits for them, and re-layouts: 6.68 us -> none  [placed(): jnp.zeros((self.n * rows,) + pieces[0][2].shape[1:], pieces[0][2].dtype)]
    unnamed x54 -> x72, local copies, waits for them, and re-layouts: 5.83 us -> 11.6 us
  transfers between devices with their start and end apart: 48 -> 47, of which waited for: 16 -> 25; matrix products, arithmetic and copies ran while one was open for 43% -> 28% of each run, Pallas kernels for 6% -> 11%
where the time goes in v2:
time: 424 us; the launch traced here: 417 us
  waiting for transfers between devices  160 us (38%)
  matrix products  88.3 us (21%)
  Pallas kernels  49.2 us (12%)
  starting transfers between devices  43.4 us (10%)
  other arithmetic  36.2 us (9%)
  local copies, waits for them, and re-layouts  25.1 us (6%)
  between operations  14.5 us (3%)
    ppermute x31, waiting for transfers between devices, to(): return lax.ppermute(arr, self.axis, pairs)  153 us
    dot_general x10, matrix products, dot(): return lax.dot_general(lhs, rhs, dims, preferred_element_type=jnp.float32)  88.3 us
    ppermute x31, starting transfers between devices, to(): return lax.ppermute(arr, self.axis, pairs)  41.5 us
    pallas_call x1, Pallas kernels, attention(): pl.pallas_call(functools.partial(attn_kernel, head_dim, q_rows), grid=(he...  26.5 us
    pallas_call x6, Pallas kernels, assemble(): pl.pallas_call(functools.partial(assemble_kernel, places, [arr.shape[0] f...  22.6 us
    unnamed x72, local copies, waits for them, and re-layouts  11.6 us
    convert_element_type x2, other arithmetic, tp_scatter(): pair = (wide(mine) + wide(other)).astype(part.dtype)  8.58 us
  transfers between devices with their start and end apart: 47, of which 25 were waited for; matrix products, arithmetic and copies ran while one was open for 28% of the time, Pallas kernels for 11%

profile of v2, /device:TPU:102, one launch (start us, length us, event | category | flops | bytes accessed | tf_op | source)
XLA Modules:
  0.0 416.7 jit_solution(1407834944870686398)
XLA Ops:
  8.1 10.5 %convolution_convert_fusion.2 = bf16[1536,1024]{1,0:T(8,128)(2,1)S(1)} fusion(bf16[2048,1024]{1,0:T(8,128)(2,1)} %param.24, bf16[1536,2048]{1,0:T(8,128)(2,1)} %param.14, f32[2048]{0:T(1024)S(1)} %convert_element_type.172, f32[1536]{0:T(1024)} %param.18, f32[1536]{0:T(1024)} %param.17), kind=kOutput, calls=%fused_computation.34 | convolution fusion | flops 6459752448 | bytes 13651968 | tf_op jit(solution)/shard_map/dot_general | solution.py:18
  20.3 9.9 %fusion.16 = f32[1024,2048]{1,0:T(8,128)} fusion(bf16[1536,2048]{1,0:T(8,128)(2,1)S(1)} %copy-done.25, bf16[1536,1024]{1,0:T(8,128)(2,1)S(1)} %convolution_convert_fusion.2), kind=kOutput, calls=%fused_computation.36 | convolution fusion | flops 6458179584 | bytes 17825792 | tf_op jit(solution)/shard_map/dot_general | solution.py:18
  30.5 13.8 %fusion.12 = bf16[1536,1024]{1,0:T(8,128)(2,1)S(1)} fusion(bf16[1536,1024]{1,0:T(8,128)(2,1)} %copy-done.33, bf16[1536,2048]{1,0:T(8,128)(2,1)} %param.21, bf16[1024,2048]{1,0:T(8,128)(2,1)} %param.25), kind=kOutput, calls=%fused_computation.28 | convolution fusion | flops 6473908224 | bytes 16777216 | tf_op jit(solution)/shard_map/dot_general | solution.py:18
  44.3 8.6 %convolution_convert_fusion.1 = bf16[1536,2048]{1,0:T(8,128)(2,1)} fusion(bf16[1536,1024]{1,0:T(8,128)(2,1)S(1)} %fusion.12, bf16[2048,1024]{1,0:T(8,128)(2,1)S(1)} %copy-done.32), kind=kOutput, calls=%fused_computation.15 | convolution fusion | flops 6445596672 | bytes 13631488 | tf_op jit(solution)/shard_map/dot_general | solution.py:18
  52.9 11.4 %fusion.36 = f32[2048,1024]{1,0:T(8,128)} fusion(bf16[1536,1024]{1,0:T(8,128)(2,1)S(1)} %fusion.12, bf16[1536,2048]{1,0:T(8,128)(2,1)} %param.14, f32[2048]{0:T(1024)S(1)} %convert_element_type.172, f32[1536]{0:T(1024)S(1)} %copy-done.28, f32[1536]{0:T(1024)S(1)} %copy-done.27), kind=kOutput, calls=%fused_computation.90 | convolution fusion | flops 6458179584 | bytes 17846272 | tf_op jit(solution)/shard_map/dot_general | solution.py:18
  64.7 4.0 dynamic-slice_bitcast_fusion.1
  68.8 5.9 %collective-permute-done = bf16[4,192,2048]{2,1,0:T(8,128)(2,1)} collective-permute-done((bf16[4,192,2048]{2,1,0:T(8,128)(2,1)}, bf16[4,192,2048]{2,1,0:T(8,128)(2,1)}, u32[]{:S(2)}, u32[]{:S(2)}) %collective-permute-start) | collective-permute-done | bytes 3145760 | tf_op jit(solution)/shard_map/ppermute | solution.py:231
  74.7 4.3 %fusion.15 = bf16[4,192,2048]{2,1,0:T(8,128)(2,1)S(1)} fusion(bf16[4,192,2048]{2,1,0:T(8,128)(2,1)} %collective-permute-done, bf16[4,2,192,2048]{3,2,1,0:T(8,128)(2,1)} %bitcast.97, s32[]{:T(128)S(6)} %select_n.50), kind=kLoop, calls=%fused_computation.33 | loop fusion | flops 6291456 | bytes 9437188 | tf_op jit(solution)/shard_map/convert_element_type | solution.py:232
  81.3 8.7 %convolution_convert_fusion.3.q_ref.k_ref.v_ref = bf16[1536,768]{1,0:T(8,128)(2,1)} fusion(bf16[768,2048]{1,0:T(8,128)(2,1)S(1)} %bitcast.94, bf16[1536,2048]{1,0:T(8,128)(2,1)} %param.13, f32[2048]{0:T(1024)S(1)} %convert_element_type.189, f32[1536]{0:T(1024)S(1)} %copy-done.30, f32[1536]{0:T(1024)S(1)} %copy-done.29), kind=kOutput, calls=%fused_computation.35 | convolution fusion | flops 4848746496 | bytes 11816960 | tf_op jit(solution)/shard_map/dot_general | solution.py:18
  94.5 3.1 collective-permute-start.3
  97.7 16.0 %collective-permute-done.4 = bf16[192,2048]{1,0:T(8,128)(2,1)} collective-permute-done((bf16[192,2048]{1,0:T(8,128)(2,1)}, bf16[192,2048]{1,0:T(8,128)(2,1)}, u32[]{:S(2)}, u32[]{:S(2)}) %collective-permute-start.4) | collective-permute-done | bytes 786464 | tf_op jit(solution)/shard_map/ppermute | solution.py:162
  116.5 4.4 %fusion.38 = (bf16[192,2048]{1,0:T(8,128)(2,1)}, f32[192,2048]{1,0:T(8,128)}) fusion(f32[192]{0:T(256)S(1)} %get-tuple-element.73, f32[192]{0:T(256)S(1)} %dynamic_slice.70, bf16[1536,2048]{1,0:T(8,128)(2,1)} %param.14, s32[]{:T(128)S(6)} %select_n.49, f32[192]{0:T(256)S(1)} %get-tuple-element.74, f32[2048]{0:T(1024)S(1)} %convert_element_type.172, ...), kind=kLoop, calls=%fused_computation.92 | loop fusion | flops 6291456 | bytes 6302728 | tf_op jit(solution)/shard_map/convert_element_type | solution.py:264
  120.9 3.8 collective-permute-start.6
  124.7 16.6 %collective-permute-done.8.refs_4_ = bf16[192,2048]{1,0:T(8,128)(2,1)S(1)} collective-permute-done((bf16[192,2048]{1,0:T(8,128)(2,1)}, bf16[192,2048]{1,0:T(8,128)(2,1)S(1)}, u32[]{:S(2)}, u32[]{:S(2)}) %collective-permute-start.8) | collective-permute-done | bytes 786464 | tf_op jit(solution)/shard_map/ppermute | solution.py:162
  144.6 3.6 collective-permute-start.10
  148.2 2.8 convert_element_type.202.refs_0_
  157.6 5.6 %assemble.6 = bf16[1536,2048]{1,0:T(8,128)(2,1)} custom-call(bf16[192,2048]{1,0:T(8,128)(2,1)} %get-tuple-element.59.refs_0_, bf16[192,2048]{1,0:T(8,128)(2,1)} %collective-permute-done.5.refs_1_, bf16[192,2048]{1,0:T(8,128)(2,1)} %copy-done.17, bf16[192,2048]{1,0:T(8,128)(2,1)} %collective-permute-done.7.refs_3_, bf16[192,2048]{1,0:T(8,128)(2,1)} %copy-done.16, ...), custom_call_target="tpu_custom_call" | custom-call | flops 3072000 | bytes 12582912 | tf_op jit(solution)/shard_map/assemble/pallas_call | solution.py:144
  163.3 5.1 %convolution_convert_fusion.4.do_ref = bf16[1536,256]{1,0:T(8,128)(2,1)S(1)} fusion(bf16[1536,2048]{1,0:T(8,128)(2,1)} %assemble.6, bf16[256,2048]{1,0:T(8,128)(2,1)} %bitcast.104), kind=kOutput, calls=%fused_computation.43 | convolution fusion | flops 1611005952 | bytes 8126464 | tf_op jit(solution)/shard_map/dot_general | solution.py:18
  168.4 26.5 %attn_fwd_bwd.1 = (bf16[1536,256]{1,0:T(8,128)(2,1)S(1)}, bf16[1536,768]{1,0:T(8,128)(2,1)S(1)}) custom-call(bf16[1536,768]{1,0:T(8,128)(2,1)} %convolution_convert_fusion.3.q_ref.k_ref.v_ref, bf16[1536,768]{1,0:T(8,128)(2,1)} %convolution_convert_fusion.3.q_ref.k_ref.v_ref, bf16[1536,768]{1,0:T(8,128)(2,1)} %convolution_convert_fusion.3.q_ref.k_ref.v_ref, ...), custom_call_target="tpu_custom_call" | custom-call | flops 14495514624 | bytes 6291456 | tf_op jit(solution)/shard_map/attn_fwd_bwd/pallas_call | solution.py:102
  197.2 7.5 %fusion.37 = f32[768,2048]{1,0:T(8,128)} fusion(bf16[1536,768]{1,0:T(8,128)(2,1)S(1)} %get-tuple-element.43, bf16[1536,2048]{1,0:T(8,128)(2,1)S(1)} %bitcast.103, f32[2048]{0:T(1024)S(1)} %convert_element_type.189, f32[1536]{0:T(1024)S(1)} %copy-done.31, f32[1536]{0:T(1024)S(1)} %copy-done.29), kind=kOutput, calls=%fused_computation.91 | convolution fusion | flops 4847566848 | bytes 14962688 | tf_op jit(solution)/shard_map/dot_general | solution.py:18
  205.0 7.0 %convolution_convert_fusion = bf16[1536,2048]{1,0:T(8,128)(2,1)S(1)} fusion(bf16[1536,768]{1,0:T(8,128)(2,1)} %copy-done.3, bf16[768,2048]{1,0:T(8,128)(2,1)S(1)} %bitcast.95), kind=kOutput, calls=%fused_computation.14 | convolution fusion | flops 4834983936 | bytes 11796480 | tf_op jit(solution)/shard_map/dot_general | solution.py:18
  212.0 3.4 copy-done.6
  217.4 6.0 %fusion.39 = f32[256,2048]{1,0:T(8,128)} fusion(bf16[1536,256]{1,0:T(8,128)(2,1)S(1)} %copy-done.2, bf16[1536,2048]{1,0:T(8,128)(2,1)} %assemble.6), kind=kOutput, calls=%fused_computation.93 | convolution fusion | flops 1610612736 | bytes 9175040 | tf_op jit(solution)/shard_map/dot_general | solution.py:18
  223.3 2.7 convert_element_type.207.refs_0_
  226.1 4.3 %fusion.14 = bf16[4,192,2048]{2,1,0:T(8,128)(2,1)S(1)} fusion(bf16[4,192,2048]{2,1,0:T(8,128)(2,1)} %collective-permute-done.14, bf16[4,2,192,2048]{3,2,1,0:T(8,128)(2,1)} %bitcast.99, s32[]{:T(128)S(6)} %select_n.50), kind=kLoop, calls=%fused_computation.31 | loop fusion | flops 6291456 | bytes 9437188 | tf_op jit(solution)/shard_map/convert_element_type | solution.py:232
  230.6 2.8 collective-permute-start.15
  233.4 9.1 %collective-permute-done.15 = bf16[96,2048]{1,0:T(8,128)(2,1)S(1)} collective-permute-done((bf16[96,2048]{1,0:T(8,128)(2,1)S(1)}, bf16[96,2048]{1,0:T(8,128)(2,1)S(1)}, u32[]{:S(2)}, u32[]{:S(2)}) %collective-permute-start.15) | collective-permute-done | bytes 393248 | tf_op jit(solution)/shard_map/ppermute | solution.py:162
  242.5 3.4 collective-permute-done.17
  248.1 3.2 collective-permute-start.16
  251.6 3.4 collective-permute-start.33
  255.0 12.7 %collective-permute-done.18 = bf16[192,2048]{1,0:T(8,128)(2,1)} collective-permute-done((bf16[192,2048]{1,0:T(8,128)(2,1)}, bf16[192,2048]{1,0:T(8,128)(2,1)}, u32[]{:S(2)}, u32[]{:S(2)}) %collective-permute-start.18) | collective-permute-done | bytes 786464 | tf_op jit(solution)/shard_map/ppermute | solution.py:162
  270.5 3.8 add_convert_fusion.refs_0_
  274.3 3.2 collective-permute-start.37
  277.5 11.4 %collective-permute-done.33.refs_2_ = bf16[256,2048]{1,0:T(8,128)(2,1)S(1)} collective-permute-done((bf16[256,2048]{1,0:T(8,128)(2,1)}, bf16[256,2048]{1,0:T(8,128)(2,1)S(1)}, u32[]{:S(2)}, u32[]{:S(2)}) %collective-permute-start.33) | collective-permute-done | bytes 1048608 | tf_op jit(solution)/shard_map/ppermute | solution.py:162
  289.4 4.9 %collective-permute-done.22.refs_4_ = bf16[192,2048]{1,0:T(8,128)(2,1)S(1)} collective-permute-done((bf16[192,2048]{1,0:T(8,128)(2,1)}, bf16[192,2048]{1,0:T(8,128)(2,1)S(1)}, u32[]{:S(2)}, u32[]{:S(2)}) %collective-permute-start.22) | collective-permute-done | bytes 786464 | tf_op jit(solution)/shard_map/ppermute | solution.py:162
  297.0 12.4 %collective-permute-done.32.refs_1_ = bf16[256,2048]{1,0:T(8,128)(2,1)S(1)} collective-permute-done((bf16[256,2048]{1,0:T(8,128)(2,1)S(1)}, bf16[256,2048]{1,0:T(8,128)(2,1)S(1)}, u32[]{:S(2)}, u32[]{:S(2)}) %collective-permute-start.32) | collective-permute-done | bytes 1048608 | tf_op jit(solution)/shard_map/ppermute | solution.py:162
  309.4 29.5 %collective-permute-done.35.refs_4_ = bf16[128,2048]{1,0:T(8,128)(2,1)S(1)} collective-permute-done((bf16[128,2048]{1,0:T(8,128)(2,1)S(1)}, bf16[128,2048]{1,0:T(8,128)(2,1)S(1)}, u32[]{:S(2)}, u32[]{:S(2)}) %collective-permute-start.35) | collective-permute-done | bytes 524320 | tf_op jit(solution)/shard_map/ppermute | solution.py:162
  346.8 3.8 collective-permute-done.26.refs_8_
  353.2 3.7 collective-permute-done.34.refs_3_
  357.4 9.1 %collective-permute-done.38.refs_3_ = bf16[256,1024]{1,0:T(8,128)(2,1)} collective-permute-done((bf16[256,1024]{1,0:T(8,128)(2,1)}, bf16[256,1024]{1,0:T(8,128)(2,1)}, u32[]{:S(2)}, u32[]{:S(2)}) %collective-permute-start.38) | collective-permute-done | bytes 524320 | tf_op jit(solution)/shard_map/ppermute | solution.py:162
  369.3 3.3 assemble.9
  372.7 3.3 assemble.10
  376.0 5.5 %assemble.7 = bf16[1536,2048]{1,0:T(8,128)(2,1)} custom-call(bf16[192,2048]{1,0:T(8,128)(2,1)} %add_convert_fusion.refs_0_, bf16[192,2048]{1,0:T(8,128)(2,1)} %collective-permute-done.19.refs_1_, bf16[192,2048]{1,0:T(8,128)(2,1)} %copy-done.15, bf16[192,2048]{1,0:T(8,128)(2,1)} %collective-permute-done.21.refs_3_, bf16[192,2048]{1,0:T(8,128)(2,1)} %copy-done.14, ...), custom_call_target="tpu_custom_call" | custom-call | flops 3072000 | bytes 12582912 | tf_op jit(solution)/shard_map/assemble/pallas_call | solution.py:144
  383.0 3.8 collective-permute-done.29.refs_2_
  391.0 2.9 collective-permute-start.41
  394.9 5.1 %collective-permute-done.31.refs_4_ = bf16[96,2048]{1,0:T(8,128)(2,1)} collective-permute-done((bf16[96,2048]{1,0:T(8,128)(2,1)S(1)}, bf16[96,2048]{1,0:T(8,128)(2,1)}, u32[]{:S(2)}, u32[]{:S(2)}) %collective-permute-start.31) | collective-permute-done | bytes 393248 | tf_op jit(solution)/shard_map/ppermute | solution.py:162
  400.0 4.0 collective-permute-done.30.refs_3_
  404.0 2.9 assemble.8
  (179 shorter events, 59.6 us)
Async XLA Ops:
  7.2 74.1 %copy-start = (bf16[2048,3,4,64]{0,3,2,1:T(8,128)(2,1)S(1)}, bf16[2048,3,4,64]{0,3,2,1:T(8,128)(2,1)}, u32[]{:S(2)}) copy-start(bf16[2048,3,4,64]{0,3,2,1:T(8,128)(2,1)} %param.22) | copy-start | bytes 9437188
  7.2 141.0 %reduce-scatter.5.cloned.1.call-start = ((), (), s32[]{:S(2)}) async-start(), calls=%async_computation.4 | async-start | bytes 10485760 | tf_op jit(solution)/shard_map/reduce_scatter | solution.py:245
  30.2 193.1 %reduce-scatter.7.cloned.1.call-start = ((), (), s32[]{:S(2)}) async-start(), calls=%async_computation.5 | async-start | bytes 10485760 | tf_op jit(solution)/shard_map/reduce_scatter | solution.py:245
  64.4 286.2 %reduce-scatter.9.cloned.1.call-start = ((), (), s32[]{:S(2)}) async-start(), calls=%async_computation.6 | async-start | bytes 7864320 | tf_op jit(solution)/shard_map/reduce_scatter | solution.py:245
  68.7 6.0 %collective-permute-start = (bf16[4,192,2048]{2,1,0:T(8,128)(2,1)}, bf16[4,192,2048]{2,1,0:T(8,128)(2,1)}, u32[]{:S(2)}, u32[]{:S(2)}) collective-permute-start(bf16[4,192,2048]{2,1,0:T(8,128)(2,1)} %dynamic-slice_bitcast_fusion.1), channel_id=1, source_target_pairs={{0,1},{1,0},{2,3},{3,2},{4,5},{5,4},{6,7},{7,6},{8,9},{9,8},{10,11... | collective-permute-start | bytes 9437192 | tf_op jit(solution)/shard_map/ppermute | solution.py:231
  79.2 11.4 %collective-permute-start.1 = (bf16[96,2048]{1,0:T(8,128)(2,1)S(1)}, bf16[96,2048]{1,0:T(8,128)(2,1)S(1)}, u32[]{:S(2)}, u32[]{:S(2)}) collective-permute-start(bf16[96,2048]{1,0:T(8,128)(2,1)S(1)} %get-tuple-element.71), channel_id=1, source_target_pairs={{0,2},{1,3},{2,4},{3,5},{4,6},{5,7},{6,0},{7,1},{8,10},{9,11},{10,... | collective-permute-start | bytes 1179656 | tf_op jit(solution)/shard_map/ppermute | solution.py:162
  79.9 12.3 %collective-permute-start.2 = (bf16[96,2048]{1,0:T(8,128)(2,1)S(1)}, bf16[96,2048]{1,0:T(8,128)(2,1)S(1)}, u32[]{:S(2)}, u32[]{:S(2)}) collective-permute-start(bf16[96,2048]{1,0:T(8,128)(2,1)S(1)} %get-tuple-element.72), channel_id=1, source_target_pairs={{0,6},{1,7},{2,0},{3,1},{4,2},{5,3},{6,4},{7,5},{8,14},{9,15},{10,... | collective-permute-start | bytes 1179656 | tf_op jit(solution)/shard_map/ppermute | solution.py:162
  93.4 20.3 %collective-permute-start.4 = (bf16[192,2048]{1,0:T(8,128)(2,1)}, bf16[192,2048]{1,0:T(8,128)(2,1)}, u32[]{:S(2)}, u32[]{:S(2)}) collective-permute-start(bf16[192,2048]{1,0:T(8,128)(2,1)} %pad_maximum_fusion.1), channel_id=1, source_target_pairs={{0,6},{1,7},{2,0},{3,1},{4,2},{5,3},{6,4},{7,5},{8,14},{9,15},{10,... | collective-permute-start | bytes 2359304 | tf_op jit(solution)/shard_map/ppermute | solution.py:162
  94.5 19.4 %collective-permute-start.3 = (bf16[192,2048]{1,0:T(8,128)(2,1)}, bf16[192,2048]{1,0:T(8,128)(2,1)}, u32[]{:S(2)}, u32[]{:S(2)}) collective-permute-start(bf16[192,2048]{1,0:T(8,128)(2,1)} %pad_maximum_fusion), channel_id=1, source_target_pairs={{0,2},{1,3},{2,4},{3,5},{4,6},{5,7},{6,0},{7,1},{8,10},{9,11},{10,... | collective-permute-start | bytes 2359304 | tf_op jit(solution)/shard_map/ppermute | solution.py:162
  120.9 20.3 %collective-permute-start.8 = (bf16[192,2048]{1,0:T(8,128)(2,1)}, bf16[192,2048]{1,0:T(8,128)(2,1)S(1)}, u32[]{:S(2)}, u32[]{:S(2)}) collective-permute-start(bf16[192,2048]{1,0:T(8,128)(2,1)} %get-tuple-element.59.refs_0_), channel_id=1, source_target_pairs={{0,6},{1,7},{2,0},{3,1},{4,2},{5,3},{6,4},{7,5},{8,14},{9,15},{10,... | collective-permute-start | bytes 2359304 | tf_op jit(solution)/shard_map/ppermute | solution.py:162
  120.9 22.0 %collective-permute-start.6 = (bf16[192,2048]{1,0:T(8,128)(2,1)}, bf16[192,2048]{1,0:T(8,128)(2,1)S(1)}, u32[]{:S(2)}, u32[]{:S(2)}) collective-permute-start(bf16[192,2048]{1,0:T(8,128)(2,1)} %get-tuple-element.59.refs_0_), channel_id=1, source_target_pairs={{0,2},{1,3},{2,4},{3,5},{4,6},{5,7},{6,0},{7,1},{8,10},{9,11},{10,... | collective-permute-start | bytes 2359304 | tf_op jit(solution)/shard_map/ppermute | solution.py:162
  124.7 30.3 %collective-permute-start.5 = (bf16[192,2048]{1,0:T(8,128)(2,1)}, bf16[192,2048]{1,0:T(8,128)(2,1)}, u32[]{:S(2)}, u32[]{:S(2)}) collective-permute-start(bf16[192,2048]{1,0:T(8,128)(2,1)} %get-tuple-element.59.refs_0_), channel_id=1, source_target_pairs={{0,1},{1,0},{2,3},{3,2},{4,5},{5,4},{6,7},{7,6},{8,9},{9,8},{10,11... | collective-permute-start | bytes 2359304 | tf_op jit(solution)/shard_map/ppermute | solution.py:241
  142.9 10.6 %collective-permute-start.12 = (bf16[96,2048]{1,0:T(8,128)(2,1)}, bf16[96,2048]{1,0:T(8,128)(2,1)S(1)}, u32[]{:S(2)}, u32[]{:S(2)}) collective-permute-start(bf16[96,2048]{1,0:T(8,128)(2,1)} %slice.125), channel_id=1, source_target_pairs={{0,6},{1,7},{2,0},{3,1},{4,2},{5,3},{6,4},{7,5},{8,14},{9,15},{10,... | collective-permute-start | bytes 1179656 | tf_op jit(solution)/shard_map/ppermute | solution.py:162
  144.6 10.4 %collective-permute-start.10 = (bf16[96,2048]{1,0:T(8,128)(2,1)}, bf16[96,2048]{1,0:T(8,128)(2,1)}, u32[]{:S(2)}, u32[]{:S(2)}) collective-permute-start(bf16[96,2048]{1,0:T(8,128)(2,1)} %slice.124), channel_id=1, source_target_pairs={{0,2},{1,3},{2,4},{3,5},{4,6},{5,7},{6,0},{7,1},{8,10},{9,11},{10,... | collective-permute-start | bytes 1179656 | tf_op jit(solution)/shard_map/ppermute | solution.py:162
  151.0 6.6 %collective-permute-start.9 = (bf16[192,2048]{1,0:T(8,128)(2,1)}, bf16[192,2048]{1,0:T(8,128)(2,1)}, u32[]{:S(2)}, u32[]{:S(2)}) collective-permute-start(bf16[192,2048]{1,0:T(8,128)(2,1)} %copy-done.16), channel_id=1, source_target_pairs={{0,1},{1,0},{2,3},{3,2},{4,5},{5,4},{6,7},{7,6},{8,9},{9,8},{10,11... | collective-permute-start | bytes 2359304 | tf_op jit(solution)/shard_map/ppermute | solution.py:241
  151.0 6.6 %collective-permute-start.7 = (bf16[192,2048]{1,0:T(8,128)(2,1)}, bf16[192,2048]{1,0:T(8,128)(2,1)}, u32[]{:S(2)}, u32[]{:S(2)}) collective-permute-start(bf16[192,2048]{1,0:T(8,128)(2,1)} %copy-done.17), channel_id=1, source_target_pairs={{0,1},{1,0},{2,3},{3,2},{4,5},{5,4},{6,7},{7,6},{8,9},{9,8},{10,11... | collective-permute-start | bytes 2359304 | tf_op jit(solution)/shard_map/ppermute | solution.py:241
  153.5 1.7 collective-permute-start.13
  154.9 1.9 collective-permute-start.11
  204.7 176.8 %reduce-scatter.11.cloned.1.call-start = ((), (), s32[]{:S(2)}) async-start(), calls=%async_computation.7 | async-start | bytes 2621440 | tf_op jit(solution)/shard_map/reduce_scatter | solution.py:245
  217.3 8.8 %collective-permute-start.14 = (bf16[4,192,2048]{2,1,0:T(8,128)(2,1)}, bf16[4,192,2048]{2,1,0:T(8,128)(2,1)}, u32[]{:S(2)}, u32[]{:S(2)}) collective-permute-start(bf16[4,192,2048]{2,1,0:T(8,128)(2,1)} %dynamic-slice_bitcast_fusion), channel_id=1, source_target_pairs={{0,1},{1,0},{2,3},{3,2},{4,5},{5,4},{6,7},{7,6},{8,9},{9,8},{10,11... | collective-permute-start | bytes 9437192 | tf_op jit(solution)/shard_map/ppermute | solution.py:231
  230.6 11.9 %collective-permute-start.15 = (bf16[96,2048]{1,0:T(8,128)(2,1)S(1)}, bf16[96,2048]{1,0:T(8,128)(2,1)S(1)}, u32[]{:S(2)}, u32[]{:S(2)}) collective-permute-start(bf16[96,2048]{1,0:T(8,128)(2,1)S(1)} %get-tuple-element.63), channel_id=1, source_target_pairs={{0,2},{1,3},{2,4},{3,5},{4,6},{5,7},{6,0},{7,1},{8,10},{9,11},{10,... | collective-permute-start | bytes 1179656 | tf_op jit(solution)/shard_map/ppermute | solution.py:162
  233.4 12.5 %collective-permute-start.17 = (bf16[96,2048]{1,0:T(8,128)(2,1)S(1)}, bf16[96,2048]{1,0:T(8,128)(2,1)S(1)}, u32[]{:S(2)}, u32[]{:S(2)}) collective-permute-start(bf16[96,2048]{1,0:T(8,128)(2,1)S(1)} %get-tuple-element.65), channel_id=1, source_target_pairs={{0,6},{1,7},{2,0},{3,1},{4,2},{5,3},{6,4},{7,5},{8,14},{9,15},{10,... | collective-permute-start | bytes 1179656 | tf_op jit(solution)/shard_map/ppermute | solution.py:162
  247.1 20.5 %collective-permute-start.18 = (bf16[192,2048]{1,0:T(8,128)(2,1)}, bf16[192,2048]{1,0:T(8,128)(2,1)}, u32[]{:S(2)}, u32[]{:S(2)}) collective-permute-start(bf16[192,2048]{1,0:T(8,128)(2,1)} %pad_maximum_fusion.3), channel_id=1, source_target_pairs={{0,6},{1,7},{2,0},{3,1},{4,2},{5,3},{6,4},{7,5},{8,14},{9,15},{10,... | collective-permute-start | bytes 2359304 | tf_op jit(solution)/shard_map/ppermute | solution.py:162
  248.1 19.8 %collective-permute-start.16 = (bf16[192,2048]{1,0:T(8,128)(2,1)}, bf16[192,2048]{1,0:T(8,128)(2,1)}, u32[]{:S(2)}, u32[]{:S(2)}) collective-permute-start(bf16[192,2048]{1,0:T(8,128)(2,1)} %pad_maximum_fusion.2), channel_id=1, source_target_pairs={{0,2},{1,3},{2,4},{3,5},{4,6},{5,7},{6,0},{7,1},{8,10},{9,11},{10,... | collective-permute-start | bytes 2359304 | tf_op jit(solution)/shard_map/ppermute | solution.py:162
  251.6 37.4 %collective-permute-start.33 = (bf16[256,2048]{1,0:T(8,128)(2,1)}, bf16[256,2048]{1,0:T(8,128)(2,1)S(1)}, u32[]{:S(2)}, u32[]{:S(2)}) collective-permute-start(bf16[256,2048]{1,0:T(8,128)(2,1)} %convert_element_type.202.refs_0_), channel_id=1, source_target_pairs={{0,24},{8,0},{16,8},{24,16},{1,25},{9,1},{17,9},{25,17},{2,26},{10... | collective-permute-start | bytes 3145736 | tf_op jit(solution)/shard_map/ppermute | solution.py:162
  274.3 20.0 %collective-permute-start.22 = (bf16[192,2048]{1,0:T(8,128)(2,1)}, bf16[192,2048]{1,0:T(8,128)(2,1)S(1)}, u32[]{:S(2)}, u32[]{:S(2)}) collective-permute-start(bf16[192,2048]{1,0:T(8,128)(2,1)} %add_convert_fusion.refs_0_), channel_id=1, source_target_pairs={{0,6},{1,7},{2,0},{3,1},{4,2},{5,3},{6,4},{7,5},{8,14},{9,15},{10,... | collective-permute-start | bytes 2359304 | tf_op jit(solution)/shard_map/ppermute | solution.py:162
  274.3 35.1 %collective-permute-start.32 = (bf16[256,2048]{1,0:T(8,128)(2,1)S(1)}, bf16[256,2048]{1,0:T(8,128)(2,1)S(1)}, u32[]{:S(2)}, u32[]{:S(2)}) collective-permute-start(bf16[256,2048]{1,0:T(8,128)(2,1)S(1)} %copy-done.8), channel_id=1, source_target_pairs={{0,8},{8,16},{16,24},{24,0},{1,9},{9,17},{17,25},{25,1},{2,10},{10... | collective-permute-start | bytes 3145736 | tf_op jit(solution)/shard_map/ppermute | solution.py:162
  274.3 66.3 %collective-permute-start.37 = (bf16[512,1024]{1,0:T(8,128)(2,1)S(1)}, bf16[512,1024]{1,0:T(8,128)(2,1)S(1)}, u32[]{:S(2)}, u32[]{:S(2)}) collective-permute-start(bf16[512,1024]{1,0:T(8,128)(2,1)S(1)} %copy-done.9), channel_id=1, source_target_pairs={{0,24},{8,0},{16,8},{24,16},{1,25},{9,1},{17,9},{25,17},{2,26},{10... | collective-permute-start | bytes 3145736 | tf_op jit(solution)/shard_map/ppermute | solution.py:162
  277.5 65.5 %collective-permute-start.36 = (bf16[512,1024]{1,0:T(8,128)(2,1)S(1)}, bf16[512,1024]{1,0:T(8,128)(2,1)S(1)}, u32[]{:S(2)}, u32[]{:S(2)}) collective-permute-start(bf16[512,1024]{1,0:T(8,128)(2,1)S(1)} %copy-done.9), channel_id=1, source_target_pairs={{0,8},{8,16},{16,24},{24,0},{1,9},{9,17},{17,25},{25,1},{2,10},{10... | collective-permute-start | bytes 3145736 | tf_op jit(solution)/shard_map/ppermute | solution.py:162
  288.9 56.7 %collective-permute-start.20 = (bf16[192,2048]{1,0:T(8,128)(2,1)}, bf16[192,2048]{1,0:T(8,128)(2,1)S(1)}, u32[]{:S(2)}, u32[]{:S(2)}) collective-permute-start(bf16[192,2048]{1,0:T(8,128)(2,1)} %add_convert_fusion.refs_0_), channel_id=1, source_target_pairs={{0,2},{1,3},{2,4},{3,5},{4,6},{5,7},{6,0},{7,1},{8,10},{9,11},{10,... | collective-permute-start | bytes 2359304 | tf_op jit(solution)/shard_map/ppermute | solution.py:162
  294.3 44.6 %collective-permute-start.35 = (bf16[128,2048]{1,0:T(8,128)(2,1)S(1)}, bf16[128,2048]{1,0:T(8,128)(2,1)S(1)}, u32[]{:S(2)}, u32[]{:S(2)}) collective-permute-start(bf16[128,2048]{1,0:T(8,128)(2,1)S(1)} %slice.131), channel_id=1, source_target_pairs={{0,24},{8,0},{16,8},{24,16},{1,25},{9,1},{17,9},{25,17},{2,26},{10... | collective-permute-start | bytes 1572872 | tf_op jit(solution)/shard_map/ppermute | solution.py:162
  309.4 57.1 %collective-permute-start.19 = (bf16[192,2048]{1,0:T(8,128)(2,1)}, bf16[192,2048]{1,0:T(8,128)(2,1)}, u32[]{:S(2)}, u32[]{:S(2)}) collective-permute-start(bf16[192,2048]{1,0:T(8,128)(2,1)} %add_convert_fusion.refs_0_), channel_id=1, source_target_pairs={{0,1},{1,0},{2,3},{3,2},{4,5},{5,4},{6,7},{7,6},{8,9},{9,8},{10,11... | collective-permute-start | bytes 2359304 | tf_op jit(solution)/shard_map/ppermute | solution.py:241
  338.9 11.7 %collective-permute-start.26 = (bf16[96,2048]{1,0:T(8,128)(2,1)S(1)}, bf16[96,2048]{1,0:T(8,128)(2,1)S(1)}, u32[]{:S(2)}, u32[]{:S(2)}) collective-permute-start(bf16[96,2048]{1,0:T(8,128)(2,1)S(1)} %slice.127), channel_id=1, source_target_pairs={{0,6},{1,7},{2,0},{3,1},{4,2},{5,3},{6,4},{7,5},{8,14},{9,15},{10,... | collective-permute-start | bytes 1179656 | tf_op jit(solution)/shard_map/ppermute | solution.py:162
  340.6 16.3 %collective-permute-start.34 = (bf16[128,2048]{1,0:T(8,128)(2,1)}, bf16[128,2048]{1,0:T(8,128)(2,1)}, u32[]{:S(2)}, u32[]{:S(2)}) collective-permute-start(bf16[128,2048]{1,0:T(8,128)(2,1)} %slice.130), channel_id=1, source_target_pairs={{0,8},{8,16},{16,24},{24,0},{1,9},{9,17},{17,25},{25,1},{2,10},{10... | collective-permute-start | bytes 1572872 | tf_op jit(solution)/shard_map/ppermute | solution.py:162
  343.0 14.0 %collective-permute-start.39 = (bf16[256,1024]{1,0:T(8,128)(2,1)}, bf16[256,1024]{1,0:T(8,128)(2,1)}, u32[]{:S(2)}, u32[]{:S(2)}) collective-permute-start(bf16[256,1024]{1,0:T(8,128)(2,1)} %slice.133), channel_id=1, source_target_pairs={{0,24},{8,0},{16,8},{24,16},{1,25},{9,1},{17,9},{25,17},{2,26},{10... | collective-permute-start | bytes 1572872 | tf_op jit(solution)/shard_map/ppermute | solution.py:162
  345.6 20.9 %collective-permute-start.38 = (bf16[256,1024]{1,0:T(8,128)(2,1)}, bf16[256,1024]{1,0:T(8,128)(2,1)}, u32[]{:S(2)}, u32[]{:S(2)}) collective-permute-start(bf16[256,1024]{1,0:T(8,128)(2,1)} %slice.132), channel_id=1, source_target_pairs={{0,8},{8,16},{16,24},{24,0},{1,9},{9,17},{17,25},{25,1},{2,10},{10... | collective-permute-start | bytes 1572872 | tf_op jit(solution)/shard_map/ppermute | solution.py:162
  350.6 16.3 %collective-permute-start.24 = (bf16[96,2048]{1,0:T(8,128)(2,1)}, bf16[96,2048]{1,0:T(8,128)(2,1)}, u32[]{:S(2)}, u32[]{:S(2)}) collective-permute-start(bf16[96,2048]{1,0:T(8,128)(2,1)} %slice.126), channel_id=1, source_target_pairs={{0,2},{1,3},{2,4},{3,5},{4,6},{5,7},{6,0},{7,1},{8,10},{9,11},{10,... | collective-permute-start | bytes 1179656 | tf_op jit(solution)/shard_map/ppermute | solution.py:162
  356.9 11.6 %collective-permute-start.27 = (bf16[96,2048]{1,0:T(8,128)(2,1)S(1)}, bf16[96,2048]{1,0:T(8,128)(2,1)S(1)}, u32[]{:S(2)}, u32[]{:S(2)}) collective-permute-start(bf16[96,2048]{1,0:T(8,128)(2,1)S(1)} %collective-permute-done.26.refs_8_), channel_id=1, source_target_pairs={{0,1},{1,0},{2,3},{3,2},{4,5},{5,4},{6,7},{7,6},{8,9},{9,8},{10,11... | collective-permute-start | bytes 1179656 | tf_op jit(solution)/shard_map/ppermute | solution.py:241
  356.9 19.1 %collective-permute-start.23 = (bf16[192,2048]{1,0:T(8,128)(2,1)}, bf16[192,2048]{1,0:T(8,128)(2,1)}, u32[]{:S(2)}, u32[]{:S(2)}) collective-permute-start(bf16[192,2048]{1,0:T(8,128)(2,1)} %copy-done.14), channel_id=1, source_target_pairs={{0,1},{1,0},{2,3},{3,2},{4,5},{5,4},{6,7},{7,6},{8,9},{9,8},{10,11... | collective-permute-start | bytes 2359304 | tf_op jit(solution)/shard_map/ppermute | solution.py:241
  366.5 9.5 %collective-permute-start.21 = (bf16[192,2048]{1,0:T(8,128)(2,1)}, bf16[192,2048]{1,0:T(8,128)(2,1)}, u32[]{:S(2)}, u32[]{:S(2)}) collective-permute-start(bf16[192,2048]{1,0:T(8,128)(2,1)} %copy-done.15), channel_id=1, source_target_pairs={{0,1},{1,0},{2,3},{3,2},{4,5},{5,4},{6,7},{7,6},{8,9},{9,8},{10,11... | collective-permute-start | bytes 2359304 | tf_op jit(solution)/shard_map/ppermute | solution.py:241
  366.5 20.3 %collective-permute-start.29 = (bf16[192,2048]{1,0:T(8,128)(2,1)}, bf16[192,2048]{1,0:T(8,128)(2,1)}, u32[]{:S(2)}, u32[]{:S(2)}) collective-permute-start(bf16[192,2048]{1,0:T(8,128)(2,1)} %convert_element_type.224.refs_0_), channel_id=1, source_target_pairs={{0,24},{8,0},{16,8},{24,16},{1,25},{9,1},{17,9},{25,17},{2,26},{10... | collective-permute-start | bytes 2359304 | tf_op jit(solution)/shard_map/ppermute | solution.py:162
  367.0 22.6 %collective-permute-start.28 = (bf16[192,2048]{1,0:T(8,128)(2,1)}, bf16[192,2048]{1,0:T(8,128)(2,1)}, u32[]{:S(2)}, u32[]{:S(2)}) collective-permute-start(bf16[192,2048]{1,0:T(8,128)(2,1)} %convert_element_type.224.refs_0_), channel_id=1, source_target_pairs={{0,8},{8,16},{16,24},{24,0},{1,9},{9,17},{17,25},{25,1},{2,10},{10... | collective-permute-start | bytes 2359304 | tf_op jit(solution)/shard_map/ppermute | solution.py:162
  369.3 6.7 %collective-permute-start.25 = (bf16[96,2048]{1,0:T(8,128)(2,1)}, bf16[96,2048]{1,0:T(8,128)(2,1)}, u32[]{:S(2)}, u32[]{:S(2)}) collective-permute-start(bf16[96,2048]{1,0:T(8,128)(2,1)} %collective-permute-done.24.refs_6_), channel_id=1, source_target_pairs={{0,1},{1,0},{2,3},{3,2},{4,5},{5,4},{6,7},{7,6},{8,9},{9,8},{10,11... | collective-permute-start | bytes 1179656 | tf_op jit(solution)/shard_map/ppermute | solution.py:241
  382.7 11.2 %collective-permute-start.40 = (bf16[64,2048]{1,0:T(8,128)(2,1)S(1)}, bf16[64,2048]{1,0:T(8,128)(2,1)}, u32[]{:S(2)}, u32[]{:S(2)}) collective-permute-start(bf16[64,2048]{1,0:T(8,128)(2,1)S(1)} %convert_element_type.225.refs_0_), channel_id=1, source_target_pairs={{0,8},{8,16},{16,24},{24,0},{1,9},{9,17},{17,25},{25,1},{2,10},{10... | collective-permute-start | bytes 786440 | tf_op jit(solution)/shard_map/ppermute | solution.py:162
  387.8 12.2 %collective-permute-start.31 = (bf16[96,2048]{1,0:T(8,128)(2,1)S(1)}, bf16[96,2048]{1,0:T(8,128)(2,1)}, u32[]{:S(2)}, u32[]{:S(2)}) collective-permute-start(bf16[96,2048]{1,0:T(8,128)(2,1)S(1)} %slice.129), channel_id=1, source_target_pairs={{0,24},{8,0},{16,8},{24,16},{1,25},{9,1},{17,9},{25,17},{2,26},{10... | collective-permute-start | bytes 1179656 | tf_op jit(solution)/shard_map/ppermute | solution.py:162
  390.6 13.4 %collective-permute-start.30 = (bf16[96,2048]{1,0:T(8,128)(2,1)S(1)}, bf16[96,2048]{1,0:T(8,128)(2,1)}, u32[]{:S(2)}, u32[]{:S(2)}) collective-permute-start(bf16[96,2048]{1,0:T(8,128)(2,1)S(1)} %slice.128), channel_id=1, source_target_pairs={{0,8},{8,16},{16,24},{24,0},{1,9},{9,17},{17,25},{25,1},{2,10},{10... | collective-permute-start | bytes 1179656 | tf_op jit(solution)/shard_map/ppermute | solution.py:162
  391.0 15.8 %collective-permute-start.41 = (bf16[64,2048]{1,0:T(8,128)(2,1)S(1)}, bf16[64,2048]{1,0:T(8,128)(2,1)}, u32[]{:S(2)}, u32[]{:S(2)}) collective-permute-start(bf16[64,2048]{1,0:T(8,128)(2,1)S(1)} %convert_element_type.225.refs_0_), channel_id=1, source_target_pairs={{0,24},{8,0},{16,8},{24,16},{1,25},{9,1},{17,9},{25,17},{2,26},{10... | collective-permute-start | bytes 786440 | tf_op jit(solution)/shard_map/ppermute | solution.py:162
  393.9 14.1 %collective-permute-start.42 = (bf16[64,2048]{1,0:T(8,128)(2,1)}, bf16[64,2048]{1,0:T(8,128)(2,1)}, u32[]{:S(2)}, u32[]{:S(2)}) collective-permute-start(bf16[64,2048]{1,0:T(8,128)(2,1)} %collective-permute-done.40.refs_1_), channel_id=1, source_target_pairs={{0,8},{8,16},{16,24},{24,0},{1,9},{9,17},{17,25},{25,1},{2,10},{10... | collective-permute-start | bytes 786440 | tf_op jit(solution)/shard_map/ppermute | solution.py:162
  (35 other events, 489.9 us)
Sparse Core Ops, SparseCore 0:
  30.3 80.7 reduce-scatter.4
  113.5 77.7 reduce-scatter.6
  204.9 74.7 reduce-scatter.8
  281.8 46.7 reduce-scatter.10

commit v3 on v2

--- a/solution.py
+++ b/solution.py
@@ -179,7 +179,7 @@
     def placed(self, pieces, rows):
         return assemble([(functools.partial(lambda offset, row: self.at(offset) * rows + row, offset, row), arr) for offset, row, arr in pieces])
 
-    def scatter(self, blocks, filler):
+    def scatter(self, blocks, filler, last=None):
         dtype = blocks.dtype
         half = blocks.shape[1] // 2
         blk = lambda d: lax.dynamic_index_in_dim(blocks, self.at(d), 0, keepdims=False)
@@ -196,6 +196,8 @@
                 go_right = (wide(go_right) + wide(right)).astype(dtype)
                 go_left = (wide(go_left) + wide(left)).astype(dtype)
             right, left = self.to(go_right, self.right), self.to(go_left, self.left)
+        if last is not None:
+            right, left = after(last, right, left)
         return wide(blk(0)) + wide(right) + wide(left)
 
 
@@ -253,7 +255,6 @@
         d_pre = (dot(dy, w_down, NT) * gelu_pair(pre_act)[1]).astype(lo)
         part_two = dot(d_pre, w_up, NT).astype(lo)
         part_up = dot(norm_two, after(part_two, d_pre), TN)
-        own_up = dp_scatter(part_up)
 
         x_in = after(part_up, x_saved)
         norm_one = (normed(x_in, mean_one, rstd_one) * wide(gain_one)).astype(lo)
@@ -262,6 +263,7 @@
         hat_cut = normed(cut(h_saved), cut(mean_two), cut(rstd_two))
         d_mid = wide(cut(grad_y)) + norm_back(d_norm_two, hat_cut, cut(rstd_two), gain_two)
         d_mid_cut = d_mid.astype(lo)
+        up_blocks = part_up.reshape(dp_ways, dim // dp_ways, part_up.shape[1])
         own_down = after(d_mid_cut, own_down).astype(lo)
         down_pieces = dp_ring.gather(own_down)
         d_mid_lo = tp_gather(d_mid_cut, own_down)
@@ -272,7 +274,7 @@
         part_one = dot(after(part_qkv, d_qkv), w_qkv_t).astype(lo)
         part_proj = dot(after(part_one, attn_out), d_mid_lo, TN)
         own_proj = dp_scatter(part_proj)
-        own_up = after(part_proj, own_up).astype(lo)
+        own_up = dp_ring.scatter(up_blocks, d_mid_cut, part_proj).astype(lo)
         up_pieces = dp_ring.gather(own_up)
         d_norm_one = tp_scatter(part_one, own_up, None)
         x_hat_cut = normed(cut(x_saved), cut(mean_one), cut(rstd_one))

time: 424 us -> 511 us (1.21)
  waiting for transfers between devices: 160 us -> 229 us
  starting transfers between devices: 43.4 us -> 55.8 us
  other arithmetic: 36.2 us -> 42.5 us
    ppermute x31 -> x35, waiting for transfers between devices: 153 us -> 227 us  [to(): return lax.ppermute(arr, self.axis, pairs)]
    ppermute x31 -> x35, starting transfers between devices: 41.5 us -> 54.2 us  [to(): return lax.ppermute(arr, self.axis, pairs)]
    ppermute x2, waiting for transfers between devices: 5.95 us -> 0.01 us  [tp_scatter(): other = after(first, lax.ppermute(other, 'tp', sibling))]
    unnamed x72 -> x82, local copies, waits for them, and re-layouts: 11.6 us -> 11.1 us
  transfers between devices with their start and end apart: 47 -> 50, of which waited for: 25 -> 25; matrix products, arithmetic and copies ran while one was open for 28% -> 22% of each run, Pallas kernels for 11% -> 3%
where the time goes in v3:
time: 511 us; the launch traced here: 505 us
  waiting for transfers between devices  229 us (45%)
  matrix products  87.8 us (17%)
  starting transfers between devices  55.8 us (11%)
  Pallas kernels  49.4 us (10%)
  other arithmetic  42.5 us (8%)
  local copies, waits for them, and re-layouts  25.7 us (5%)
  between operations  14.7 us (3%)
    ppermute x35, waiting for transfers between devices, to(): return lax.ppermute(arr, self.axis, pairs)  227 us
    dot_general x10, matrix products, dot(): return lax.dot_general(lhs, rhs, dims, preferred_element_type=jnp.float32)  87.8 us
    ppermute x35, starting transfers between devices, to(): return lax.ppermute(arr, self.axis, pairs)  54.2 us
    pallas_call x1, Pallas kernels, attention(): pl.pallas_call(functools.partial(attn_kernel, head_dim, q_rows), grid=(he...  26.9 us
    pallas_call x6, Pallas kernels, assemble(): pl.pallas_call(functools.partial(assemble_kernel, places, [arr.shape[0] f...  22.5 us
    unnamed x82, local copies, waits for them, and re-layouts  11.1 us
  transfers between devices with their start and end apart: 50, of which 25 were waited for; matrix products, arithmetic and copies ran while one was open for 22% of the time, Pallas kernels for 3%

profile of v3, /device:TPU:102, one launch (start us, length us, event | category | flops | bytes accessed | tf_op | source)
XLA Modules:
  0.0 504.7 jit_solution(6085323152116304340)
XLA Ops:
  8.1 10.5 %convolution_convert_fusion.2 = bf16[1536,1024]{1,0:T(8,128)(2,1)S(1)} fusion(bf16[2048,1024]{1,0:T(8,128)(2,1)} %param.24, bf16[1536,2048]{1,0:T(8,128)(2,1)} %param.14, f32[2048]{0:T(1024)S(1)} %convert_element_type.172, f32[1536]{0:T(1024)} %param.18, f32[1536]{0:T(1024)} %param.17), kind=kOutput, calls=%fused_computation.34 | convolution fusion | flops 6459752448 | bytes 13651968 | tf_op jit(solution)/shard_map/dot_general | solution.py:18
  20.3 9.9 %fusion.16 = f32[1024,2048]{1,0:T(8,128)} fusion(bf16[1536,2048]{1,0:T(8,128)(2,1)S(1)} %copy-done.29, bf16[1536,1024]{1,0:T(8,128)(2,1)S(1)} %convolution_convert_fusion.2), kind=kOutput, calls=%fused_computation.36 | convolution fusion | flops 6458179584 | bytes 17825792 | tf_op jit(solution)/shard_map/dot_general | solution.py:18
  30.5 13.8 %fusion.12 = bf16[1536,1024]{1,0:T(8,128)(2,1)S(1)} fusion(bf16[1536,1024]{1,0:T(8,128)(2,1)} %copy-done.37, bf16[1536,2048]{1,0:T(8,128)(2,1)} %param.21, bf16[1024,2048]{1,0:T(8,128)(2,1)} %param.25), kind=kOutput, calls=%fused_computation.28 | convolution fusion | flops 6473908224 | bytes 16777216 | tf_op jit(solution)/shard_map/dot_general | solution.py:18
  44.3 7.1 %convolution_convert_fusion.1 = bf16[1536,2048]{1,0:T(8,128)(2,1)S(1)} fusion(bf16[1536,1024]{1,0:T(8,128)(2,1)S(1)} %fusion.12, bf16[2048,1024]{1,0:T(8,128)(2,1)S(1)} %copy-done.36), kind=kOutput, calls=%fused_computation.15 | convolution fusion | flops 6445596672 | bytes 13631488 | tf_op jit(solution)/shard_map/dot_general | solution.py:18
  55.1 13.7 %fusion.40 = f32[2048,1024]{1,0:T(8,128)} fusion(bf16[1536,1024]{1,0:T(8,128)(2,1)} %copy-done.38, bf16[1536,2048]{1,0:T(8,128)(2,1)} %param.14, f32[2048]{0:T(1024)S(1)} %convert_element_type.172, f32[1536]{0:T(1024)S(1)} %copy-done.31, f32[1536]{0:T(1024)S(1)} %copy-done.32), kind=kOutput, calls=%fused_computation.103 | convolution fusion | flops 6458179584 | bytes 17846272 | tf_op jit(solution)/shard_map/dot_general | solution.py:18
  68.9 4.3 fusion.15
  75.6 8.7 %convolution_convert_fusion.3.q_ref.k_ref.v_ref = bf16[1536,768]{1,0:T(8,128)(2,1)} fusion(bf16[768,2048]{1,0:T(8,128)(2,1)S(1)} %bitcast.117, bf16[1536,2048]{1,0:T(8,128)(2,1)} %param.13, f32[2048]{0:T(1024)S(1)} %convert_element_type.189, f32[1536]{0:T(1024)S(1)} %copy-done.33, f32[1536]{0:T(1024)S(1)} %copy-done.34), kind=kOutput, calls=%fused_computation.35 | convolution fusion | flops 4848746496 | bytes 11816960 | tf_op jit(solution)/shard_map/dot_general | solution.py:18
  89.0 3.1 collective-permute-start.3
  92.3 16.3 %collective-permute-done.4 = bf16[192,2048]{1,0:T(8,128)(2,1)} collective-permute-done((bf16[192,2048]{1,0:T(8,128)(2,1)}, bf16[192,2048]{1,0:T(8,128)(2,1)}, u32[]{:S(2)}, u32[]{:S(2)}) %collective-permute-start.4) | collective-permute-done | bytes 786464 | tf_op jit(solution)/shard_map/ppermute | solution.py:162
  111.3 4.4 fusion.42
  115.7 3.7 collective-permute-start.6
  119.4 15.8 %collective-permute-done.6.refs_2_ = bf16[192,2048]{1,0:T(8,128)(2,1)S(1)} collective-permute-done((bf16[192,2048]{1,0:T(8,128)(2,1)}, bf16[192,2048]{1,0:T(8,128)(2,1)S(1)}, u32[]{:S(2)}, u32[]{:S(2)}) %collective-permute-start.6) | collective-permute-done | bytes 786464 | tf_op jit(solution)/shard_map/ppermute | solution.py:162
  136.9 3.6 collective-permute-start.10
  142.2 2.8 convert_element_type.202.refs_0_
  147.0 5.1 %collective-permute-done.12.refs_8_ = bf16[96,2048]{1,0:T(8,128)(2,1)} collective-permute-done((bf16[96,2048]{1,0:T(8,128)(2,1)}, bf16[96,2048]{1,0:T(8,128)(2,1)}, u32[]{:S(2)}, u32[]{:S(2)}) %collective-permute-start.12) | collective-permute-done | bytes 393248 | tf_op jit(solution)/shard_map/ppermute | solution.py:162
  155.7 5.5 %assemble.6 = bf16[1536,2048]{1,0:T(8,128)(2,1)} custom-call(bf16[192,2048]{1,0:T(8,128)(2,1)} %get-tuple-element.65.refs_0_, bf16[192,2048]{1,0:T(8,128)(2,1)} %collective-permute-done.5.refs_1_, bf16[192,2048]{1,0:T(8,128)(2,1)} %copy-done.17, bf16[192,2048]{1,0:T(8,128)(2,1)} %copy-done.22, bf16[192,2048]{1,0:T(8,128)(2,1)} %copy-done.19, ...), custom_call_target="tpu_custom_call" | custom-call | flops 3072000 | bytes 12582912 | tf_op jit(solution)/shard_map/assemble/pallas_call | solution.py:144
  161.2 5.0 convolution_convert_fusion.4.do_ref
  166.2 26.9 %attn_fwd_bwd.1 = (bf16[1536,256]{1,0:T(8,128)(2,1)S(1)}, bf16[1536,768]{1,0:T(8,128)(2,1)S(1)}) custom-call(bf16[1536,768]{1,0:T(8,128)(2,1)} %convolution_convert_fusion.3.q_ref.k_ref.v_ref, bf16[1536,768]{1,0:T(8,128)(2,1)} %convolution_convert_fusion.3.q_ref.k_ref.v_ref, bf16[1536,768]{1,0:T(8,128)(2,1)} %convolution_convert_fusion.3.q_ref.k_ref.v_ref, ...), custom_call_target="tpu_custom_call" | custom-call | flops 14495514624 | bytes 6291456 | tf_op jit(solution)/shard_map/attn_fwd_bwd/pallas_call | solution.py:102
  195.5 7.3 %fusion.41 = f32[768,2048]{1,0:T(8,128)} fusion(bf16[1536,768]{1,0:T(8,128)(2,1)S(1)} %get-tuple-element.46, bf16[1536,2048]{1,0:T(8,128)(2,1)S(1)} %bitcast.129, f32[2048]{0:T(1024)S(1)} %convert_element_type.189, f32[1536]{0:T(1024)S(1)} %copy-done.33, f32[1536]{0:T(1024)S(1)} %copy-done.35), kind=kOutput, calls=%fused_computation.104 | convolution fusion | flops 4847566848 | bytes 14962688 | tf_op jit(solution)/shard_map/dot_general | solution.py:18
  206.6 4.2 collective-permute-start.15
  210.9 5.5 %convolution_convert_fusion = bf16[1536,2048]{1,0:T(8,128)(2,1)S(1)} fusion(bf16[1536,768]{1,0:T(8,128)(2,1)S(1)} %copy-done.3, bf16[768,2048]{1,0:T(8,128)(2,1)S(1)} %bitcast.118), kind=kOutput, calls=%fused_computation.14 | convolution fusion | flops 4834983936 | bytes 11796480 | tf_op jit(solution)/shard_map/dot_general | solution.py:18
  220.0 33.8 %collective-permute-done.14 = f32[256,1024]{1,0:T(8,128)S(1)} collective-permute-done((f32[256,1024]{1,0:T(8,128)S(1)}, f32[256,1024]{1,0:T(8,128)S(1)}, u32[]{:S(2)}, u32[]{:S(2)}) %collective-permute-start.14) | collective-permute-done | bytes 1048608 | tf_op jit(solution)/shard_map/ppermute | solution.py:162
  260.9 3.6 collective-permute-start.17
  264.5 6.3 %fusion.43 = f32[256,2048]{1,0:T(8,128)} fusion(bf16[1536,256]{1,0:T(8,128)(2,1)} %copy-done.1, bf16[1536,2048]{1,0:T(8,128)(2,1)} %assemble.6), kind=kOutput, calls=%fused_computation.106 | convolution fusion | flops 1610612736 | bytes 9175040 | tf_op jit(solution)/shard_map/dot_general | solution.py:18
  270.8 59.1 %collective-permute-done.16 = f32[512,1024]{1,0:T(8,128)} collective-permute-done((f32[512,1024]{1,0:T(8,128)}, f32[512,1024]{1,0:T(8,128)}, u32[]{:S(2)}, u32[]{:S(2)}) %collective-permute-start.16) | collective-permute-done | bytes 2097184 | tf_op jit(solution)/shard_map/ppermute | solution.py:162
  329.9 4.4 fusion.23.refs_0_
  334.2 4.2 fusion.14
  340.7 8.2 %collective-permute-done.19 = bf16[96,2048]{1,0:T(8,128)(2,1)S(1)} collective-permute-done((bf16[96,2048]{1,0:T(8,128)(2,1)S(1)}, bf16[96,2048]{1,0:T(8,128)(2,1)S(1)}, u32[]{:S(2)}, u32[]{:S(2)}) %collective-permute-start.19) | collective-permute-done | bytes 393248 | tf_op jit(solution)/shard_map/ppermute | solution.py:162
  352.8 2.8 collective-permute-start.20
  356.9 13.8 %collective-permute-done.22 = bf16[192,2048]{1,0:T(8,128)(2,1)} collective-permute-done((bf16[192,2048]{1,0:T(8,128)(2,1)}, bf16[192,2048]{1,0:T(8,128)(2,1)}, u32[]{:S(2)}, u32[]{:S(2)}) %collective-permute-start.22) | collective-permute-done | bytes 786464 | tf_op jit(solution)/shard_map/ppermute | solution.py:162
  373.6 3.8 add_convert_fusion.refs_0_
  377.4 3.7 collective-permute-start.24
  381.1 2.9 collective-permute-start.37
  384.0 3.2 collective-permute-start.41
  387.2 13.0 %collective-permute-done.36.refs_1_ = bf16[256,2048]{1,0:T(8,128)(2,1)S(1)} collective-permute-done((bf16[256,2048]{1,0:T(8,128)(2,1)}, bf16[256,2048]{1,0:T(8,128)(2,1)S(1)}, u32[]{:S(2)}, u32[]{:S(2)}) %collective-permute-start.36) | collective-permute-done | bytes 1048608 | tf_op jit(solution)/shard_map/ppermute | solution.py:162
  400.4 10.4 %collective-permute-done.37.refs_2_ = bf16[256,2048]{1,0:T(8,128)(2,1)S(1)} collective-permute-done((bf16[256,2048]{1,0:T(8,128)(2,1)S(1)}, bf16[256,2048]{1,0:T(8,128)(2,1)S(1)}, u32[]{:S(2)}, u32[]{:S(2)}) %collective-permute-start.37) | collective-permute-done | bytes 1048608 | tf_op jit(solution)/shard_map/ppermute | solution.py:162
  410.8 19.9 %collective-permute-done.38.refs_3_ = bf16[128,2048]{1,0:T(8,128)(2,1)S(1)} collective-permute-done((bf16[128,2048]{1,0:T(8,128)(2,1)S(1)}, bf16[128,2048]{1,0:T(8,128)(2,1)S(1)}, u32[]{:S(2)}, u32[]{:S(2)}) %collective-permute-start.38) | collective-permute-done | bytes 524320 | tf_op jit(solution)/shard_map/ppermute | solution.py:162
  435.6 2.9 collective-permute-start.43
  443.6 3.3 collective-permute-done.39.refs_4_
  447.4 6.7 %collective-permute-done.43.refs_4_ = bf16[256,1024]{1,0:T(8,128)(2,1)} collective-permute-done((bf16[256,1024]{1,0:T(8,128)(2,1)}, bf16[256,1024]{1,0:T(8,128)(2,1)}, u32[]{:S(2)}, u32[]{:S(2)}) %collective-permute-start.43) | collective-permute-done | bytes 524320 | tf_op jit(solution)/shard_map/ppermute | solution.py:162
  454.6 3.1 collective-permute-start.33
  458.7 3.3 assemble.9
  462.0 3.3 assemble.10
  465.3 5.5 %assemble.7 = bf16[1536,2048]{1,0:T(8,128)(2,1)} custom-call(bf16[192,2048]{1,0:T(8,128)(2,1)} %add_convert_fusion.refs_0_, bf16[192,2048]{1,0:T(8,128)(2,1)} %collective-permute-done.23.refs_1_, bf16[192,2048]{1,0:T(8,128)(2,1)} %copy-done.15, bf16[192,2048]{1,0:T(8,128)(2,1)} %collective-permute-done.25.refs_3_, bf16[192,2048]{1,0:T(8,128)(2,1)} %copy-done.16, ...), custom_call_target="tpu_custom_call" | custom-call | flops 3072000 | bytes 12582912 | tf_op jit(solution)/shard_map/assemble/pallas_call | solution.py:144
  472.1 4.0 collective-permute-done.32.refs_1_
  478.3 3.3 collective-permute-start.35
  483.6 7.4 %collective-permute-done.34.refs_3_ = bf16[96,2048]{1,0:T(8,128)(2,1)} collective-permute-done((bf16[96,2048]{1,0:T(8,128)(2,1)S(1)}, bf16[96,2048]{1,0:T(8,128)(2,1)}, u32[]{:S(2)}, u32[]{:S(2)}) %collective-permute-start.34) | collective-permute-done | bytes 393248 | tf_op jit(solution)/shard_map/ppermute | solution.py:162
  491.1 2.9 assemble.8
  (198 shorter events, 74.0 us)
Async XLA Ops:
  7.2 135.0 %reduce-scatter.4.cloned.1.call-start = ((), (), s32[]{:S(2)}) async-start(), calls=%async_computation.3 | async-start | bytes 10485760 | tf_op jit(solution)/shard_map/reduce_scatter | solution.py:247
  30.2 411.0 %reduce-scatter.6.cloned.1.call-start = ((), (), s32[]{:S(2)}) async-start(), calls=%async_computation.4 | async-start | bytes 7864320 | tf_op jit(solution)/shard_map/reduce_scatter | solution.py:247
  55.1 13.8 %collective-permute-start = (bf16[4,192,2048]{2,1,0:T(8,128)(2,1)}, bf16[4,192,2048]{2,1,0:T(8,128)(2,1)}, u32[]{:S(2)}, u32[]{:S(2)}) collective-permute-start(bf16[4,192,2048]{2,1,0:T(8,128)(2,1)} %dynamic-slice_bitcast_fusion.1), channel_id=1, source_target_pairs={{0,1},{1,0},{2,3},{3,2},{4,5},{5,4},{6,7},{7,6},{8,9},{9,8},{10,11... | collective-permute-start | bytes 9437192 | tf_op jit(solution)/shard_map/ppermute | solution.py:233
  73.4 11.7 %collective-permute-start.1 = (bf16[96,2048]{1,0:T(8,128)(2,1)S(1)}, bf16[96,2048]{1,0:T(8,128)(2,1)S(1)}, u32[]{:S(2)}, u32[]{:S(2)}) collective-permute-start(bf16[96,2048]{1,0:T(8,128)(2,1)S(1)} %get-tuple-element.83), channel_id=1, source_target_pairs={{0,2},{1,3},{2,4},{3,5},{4,6},{5,7},{6,0},{7,1},{8,10},{9,11},{10,... | collective-permute-start | bytes 1179656 | tf_op jit(solution)/shard_map/ppermute | solution.py:162
  74.1 12.6 %collective-permute-start.2 = (bf16[96,2048]{1,0:T(8,128)(2,1)S(1)}, bf16[96,2048]{1,0:T(8,128)(2,1)S(1)}, u32[]{:S(2)}, u32[]{:S(2)}) collective-permute-start(bf16[96,2048]{1,0:T(8,128)(2,1)S(1)} %get-tuple-element.84), channel_id=1, source_target_pairs={{0,6},{1,7},{2,0},{3,1},{4,2},{5,3},{6,4},{7,5},{8,14},{9,15},{10,... | collective-permute-start | bytes 1179656 | tf_op jit(solution)/shard_map/ppermute | solution.py:162
  88.0 20.6 %collective-permute-start.4 = (bf16[192,2048]{1,0:T(8,128)(2,1)}, bf16[192,2048]{1,0:T(8,128)(2,1)}, u32[]{:S(2)}, u32[]{:S(2)}) collective-permute-start(bf16[192,2048]{1,0:T(8,128)(2,1)} %pad_maximum_fusion.3), channel_id=1, source_target_pairs={{0,6},{1,7},{2,0},{3,1},{4,2},{5,3},{6,4},{7,5},{8,14},{9,15},{10,... | collective-permute-start | bytes 2359304 | tf_op jit(solution)/shard_map/ppermute | solution.py:162
  89.0 19.7 %collective-permute-start.3 = (bf16[192,2048]{1,0:T(8,128)(2,1)}, bf16[192,2048]{1,0:T(8,128)(2,1)}, u32[]{:S(2)}, u32[]{:S(2)}) collective-permute-start(bf16[192,2048]{1,0:T(8,128)(2,1)} %pad_maximum_fusion.2), channel_id=1, source_target_pairs={{0,2},{1,3},{2,4},{3,5},{4,6},{5,7},{6,0},{7,1},{8,10},{9,11},{10,... | collective-permute-start | bytes 2359304 | tf_op jit(solution)/shard_map/ppermute | solution.py:162
  115.7 19.5 %collective-permute-start.6 = (bf16[192,2048]{1,0:T(8,128)(2,1)}, bf16[192,2048]{1,0:T(8,128)(2,1)S(1)}, u32[]{:S(2)}, u32[]{:S(2)}) collective-permute-start(bf16[192,2048]{1,0:T(8,128)(2,1)} %get-tuple-element.65.refs_0_), channel_id=1, source_target_pairs={{0,2},{1,3},{2,4},{3,5},{4,6},{5,7},{6,0},{7,1},{8,10},{9,11},{10,... | collective-permute-start | bytes 2359304 | tf_op jit(solution)/shard_map/ppermute | solution.py:162
  119.4 21.0 %collective-permute-start.8 = (bf16[192,2048]{1,0:T(8,128)(2,1)}, bf16[192,2048]{1,0:T(8,128)(2,1)S(1)}, u32[]{:S(2)}, u32[]{:S(2)}) collective-permute-start(bf16[192,2048]{1,0:T(8,128)(2,1)} %get-tuple-element.65.refs_0_), channel_id=1, source_target_pairs={{0,6},{1,7},{2,0},{3,1},{4,2},{5,3},{6,4},{7,5},{8,14},{9,15},{10,... | collective-permute-start | bytes 2359304 | tf_op jit(solution)/shard_map/ppermute | solution.py:162
  119.4 32.7 %collective-permute-start.5 = (bf16[192,2048]{1,0:T(8,128)(2,1)}, bf16[192,2048]{1,0:T(8,128)(2,1)}, u32[]{:S(2)}, u32[]{:S(2)}) collective-permute-start(bf16[192,2048]{1,0:T(8,128)(2,1)} %get-tuple-element.65.refs_0_), channel_id=1, source_target_pairs={{0,1},{1,0},{2,3},{3,2},{4,5},{5,4},{6,7},{7,6},{8,9},{9,8},{10,11... | collective-permute-start | bytes 2359304 | tf_op jit(solution)/shard_map/ppermute | solution.py:243
  136.9 10.1 %collective-permute-start.10 = (bf16[96,2048]{1,0:T(8,128)(2,1)}, bf16[96,2048]{1,0:T(8,128)(2,1)S(1)}, u32[]{:S(2)}, u32[]{:S(2)}) collective-permute-start(bf16[96,2048]{1,0:T(8,128)(2,1)} %slice.172), channel_id=1, source_target_pairs={{0,2},{1,3},{2,4},{3,5},{4,6},{5,7},{6,0},{7,1},{8,10},{9,11},{10,... | collective-permute-start | bytes 1179656 | tf_op jit(solution)/shard_map/ppermute | solution.py:162
  142.2 9.9 %collective-permute-start.12 = (bf16[96,2048]{1,0:T(8,128)(2,1)}, bf16[96,2048]{1,0:T(8,128)(2,1)}, u32[]{:S(2)}, u32[]{:S(2)}) collective-permute-start(bf16[96,2048]{1,0:T(8,128)(2,1)} %slice.173), channel_id=1, source_target_pairs={{0,6},{1,7},{2,0},{3,1},{4,2},{5,3},{6,4},{7,5},{8,14},{9,15},{10,... | collective-permute-start | bytes 1179656 | tf_op jit(solution)/shard_map/ppermute | solution.py:162
  145.0 9.0 %collective-permute-start.7 = (bf16[192,2048]{1,0:T(8,128)(2,1)S(1)}, bf16[192,2048]{1,0:T(8,128)(2,1)S(1)}, u32[]{:S(2)}, u32[]{:S(2)}) collective-permute-start(bf16[192,2048]{1,0:T(8,128)(2,1)S(1)} %copy-done.18), channel_id=1, source_target_pairs={{0,1},{1,0},{2,3},{3,2},{4,5},{5,4},{6,7},{7,6},{8,9},{9,8},{10,11... | collective-permute-start | bytes 2359304 | tf_op jit(solution)/shard_map/ppermute | solution.py:243
  145.0 10.6 %collective-permute-start.9 = (bf16[192,2048]{1,0:T(8,128)(2,1)S(1)}, bf16[192,2048]{1,0:T(8,128)(2,1)}, u32[]{:S(2)}, u32[]{:S(2)}) collective-permute-start(bf16[192,2048]{1,0:T(8,128)(2,1)S(1)} %copy-done.20), channel_id=1, source_target_pairs={{0,1},{1,0},{2,3},{3,2},{4,5},{5,4},{6,7},{7,6},{8,9},{9,8},{10,11... | collective-permute-start | bytes 2359304 | tf_op jit(solution)/shard_map/ppermute | solution.py:243
  202.9 268.0 %reduce-scatter.8.cloned.1.call-start = ((), (), s32[]{:S(2)}) async-start(), calls=%async_computation.5 | async-start | bytes 2621440 | tf_op jit(solution)/shard_map/reduce_scatter | solution.py:247
  205.7 48.1 %collective-permute-start.14 = (f32[256,1024]{1,0:T(8,128)S(1)}, f32[256,1024]{1,0:T(8,128)S(1)}, u32[]{:S(2)}, u32[]{:S(2)}) collective-permute-start(f32[256,1024]{1,0:T(8,128)S(1)} %get-tuple-element.68), channel_id=1, source_target_pairs={{0,8},{8,16},{16,24},{24,0},{1,9},{9,17},{17,25},{25,1},{2,10},{10... | collective-permute-start | bytes 3145736 | tf_op jit(solution)/shard_map/ppermute | solution.py:162
  206.6 49.3 %collective-permute-start.15 = (f32[256,1024]{1,0:T(8,128)S(1)}, f32[256,1024]{1,0:T(8,128)S(1)}, u32[]{:S(2)}, u32[]{:S(2)}) collective-permute-start(f32[256,1024]{1,0:T(8,128)S(1)} %get-tuple-element.69), channel_id=1, source_target_pairs={{0,24},{8,0},{16,8},{24,16},{1,25},{9,1},{17,9},{25,17},{2,26},{10... | collective-permute-start | bytes 3145736 | tf_op jit(solution)/shard_map/ppermute | solution.py:162
  220.0 114.2 %collective-permute-start.18 = (bf16[4,192,2048]{2,1,0:T(8,128)(2,1)}, bf16[4,192,2048]{2,1,0:T(8,128)(2,1)}, u32[]{:S(2)}, u32[]{:S(2)}) collective-permute-start(bf16[4,192,2048]{2,1,0:T(8,128)(2,1)} %dynamic-slice_bitcast_fusion), channel_id=1, source_target_pairs={{0,1},{1,0},{2,3},{3,2},{4,5},{5,4},{6,7},{7,6},{8,9},{9,8},{10,11... | collective-permute-start | bytes 9437192 | tf_op jit(solution)/shard_map/ppermute | solution.py:233
  259.4 70.5 %collective-permute-start.16 = (f32[512,1024]{1,0:T(8,128)}, f32[512,1024]{1,0:T(8,128)}, u32[]{:S(2)}, u32[]{:S(2)}) collective-permute-start(f32[512,1024]{1,0:T(8,128)} %pad_maximum_fusion), channel_id=1, source_target_pairs={{0,8},{8,16},{16,24},{24,0},{1,9},{9,17},{17,25},{25,1},{2,10},{10... | collective-permute-start | bytes 6291464 | tf_op jit(solution)/shard_map/ppermute | solution.py:162
  260.9 68.9 %collective-permute-start.17 = (f32[512,1024]{1,0:T(8,128)}, f32[512,1024]{1,0:T(8,128)}, u32[]{:S(2)}, u32[]{:S(2)}) collective-permute-start(f32[512,1024]{1,0:T(8,128)} %pad_maximum_fusion.1), channel_id=1, source_target_pairs={{0,24},{8,0},{16,8},{24,16},{1,25},{9,1},{17,9},{25,17},{2,26},{10... | collective-permute-start | bytes 6291464 | tf_op jit(solution)/shard_map/ppermute | solution.py:162
  338.6 10.3 %collective-permute-start.19 = (bf16[96,2048]{1,0:T(8,128)(2,1)S(1)}, bf16[96,2048]{1,0:T(8,128)(2,1)S(1)}, u32[]{:S(2)}, u32[]{:S(2)}) collective-permute-start(bf16[96,2048]{1,0:T(8,128)(2,1)S(1)} %get-tuple-element.75), channel_id=1, source_target_pairs={{0,2},{1,3},{2,4},{3,5},{4,6},{5,7},{6,0},{7,1},{8,10},{9,11},{10,... | collective-permute-start | bytes 1179656 | tf_op jit(solution)/shard_map/ppermute | solution.py:162
  338.7 11.5 %collective-permute-start.21 = (bf16[96,2048]{1,0:T(8,128)(2,1)S(1)}, bf16[96,2048]{1,0:T(8,128)(2,1)S(1)}, u32[]{:S(2)}, u32[]{:S(2)}) collective-permute-start(bf16[96,2048]{1,0:T(8,128)(2,1)S(1)} %get-tuple-element.77), channel_id=1, source_target_pairs={{0,6},{1,7},{2,0},{3,1},{4,2},{5,3},{6,4},{7,5},{8,14},{9,15},{10,... | collective-permute-start | bytes 1179656 | tf_op jit(solution)/shard_map/ppermute | solution.py:162
  351.4 19.3 %collective-permute-start.22 = (bf16[192,2048]{1,0:T(8,128)(2,1)}, bf16[192,2048]{1,0:T(8,128)(2,1)}, u32[]{:S(2)}, u32[]{:S(2)}) collective-permute-start(bf16[192,2048]{1,0:T(8,128)(2,1)} %pad_maximum_fusion.5), channel_id=1, source_target_pairs={{0,6},{1,7},{2,0},{3,1},{4,2},{5,3},{6,4},{7,5},{8,14},{9,15},{10,... | collective-permute-start | bytes 2359304 | tf_op jit(solution)/shard_map/ppermute | solution.py:162
  352.8 18.1 %collective-permute-start.20 = (bf16[192,2048]{1,0:T(8,128)(2,1)}, bf16[192,2048]{1,0:T(8,128)(2,1)}, u32[]{:S(2)}, u32[]{:S(2)}) collective-permute-start(bf16[192,2048]{1,0:T(8,128)(2,1)} %pad_maximum_fusion.4), channel_id=1, source_target_pairs={{0,2},{1,3},{2,4},{3,5},{4,6},{5,7},{6,0},{7,1},{8,10},{9,11},{10,... | collective-permute-start | bytes 2359304 | tf_op jit(solution)/shard_map/ppermute | solution.py:162
  355.9 44.3 %collective-permute-start.36 = (bf16[256,2048]{1,0:T(8,128)(2,1)}, bf16[256,2048]{1,0:T(8,128)(2,1)S(1)}, u32[]{:S(2)}, u32[]{:S(2)}) collective-permute-start(bf16[256,2048]{1,0:T(8,128)(2,1)} %convert_element_type.202.refs_0_), channel_id=1, source_target_pairs={{0,8},{8,16},{16,24},{24,0},{1,9},{9,17},{17,25},{25,1},{2,10},{10... | collective-permute-start | bytes 3145736 | tf_op jit(solution)/shard_map/ppermute | solution.py:162
  377.4 22.9 %collective-permute-start.24 = (bf16[192,2048]{1,0:T(8,128)(2,1)}, bf16[192,2048]{1,0:T(8,128)(2,1)S(1)}, u32[]{:S(2)}, u32[]{:S(2)}) collective-permute-start(bf16[192,2048]{1,0:T(8,128)(2,1)} %add_convert_fusion.refs_0_), channel_id=1, source_target_pairs={{0,2},{1,3},{2,4},{3,5},{4,6},{5,7},{6,0},{7,1},{8,10},{9,11},{10,... | collective-permute-start | bytes 2359304 | tf_op jit(solution)/shard_map/ppermute | solution.py:162
  381.1 29.7 %collective-permute-start.37 = (bf16[256,2048]{1,0:T(8,128)(2,1)S(1)}, bf16[256,2048]{1,0:T(8,128)(2,1)S(1)}, u32[]{:S(2)}, u32[]{:S(2)}) collective-permute-start(bf16[256,2048]{1,0:T(8,128)(2,1)S(1)} %copy-done.9), channel_id=1, source_target_pairs={{0,24},{8,0},{16,8},{24,16},{1,25},{9,1},{17,9},{25,17},{2,26},{10... | collective-permute-start | bytes 3145736 | tf_op jit(solution)/shard_map/ppermute | solution.py:162
  384.0 47.8 %collective-permute-start.40 = (bf16[512,1024]{1,0:T(8,128)(2,1)S(1)}, bf16[512,1024]{1,0:T(8,128)(2,1)S(1)}, u32[]{:S(2)}, u32[]{:S(2)}) collective-permute-start(bf16[512,1024]{1,0:T(8,128)(2,1)S(1)} %copy-done.10), channel_id=1, source_target_pairs={{0,8},{8,16},{16,24},{24,0},{1,9},{9,17},{17,25},{25,1},{2,10},{10... | collective-permute-start | bytes 3145736 | tf_op jit(solution)/shard_map/ppermute | solution.py:162
  384.0 50.3 %collective-permute-start.41 = (bf16[512,1024]{1,0:T(8,128)(2,1)S(1)}, bf16[512,1024]{1,0:T(8,128)(2,1)S(1)}, u32[]{:S(2)}, u32[]{:S(2)}) collective-permute-start(bf16[512,1024]{1,0:T(8,128)(2,1)S(1)} %copy-done.10), channel_id=1, source_target_pairs={{0,24},{8,0},{16,8},{24,16},{1,25},{9,1},{17,9},{25,17},{2,26},{10... | collective-permute-start | bytes 3145736 | tf_op jit(solution)/shard_map/ppermute | solution.py:162
  400.2 35.4 %collective-permute-start.26 = (bf16[192,2048]{1,0:T(8,128)(2,1)}, bf16[192,2048]{1,0:T(8,128)(2,1)S(1)}, u32[]{:S(2)}, u32[]{:S(2)}) collective-permute-start(bf16[192,2048]{1,0:T(8,128)(2,1)} %add_convert_fusion.refs_0_), channel_id=1, source_target_pairs={{0,6},{1,7},{2,0},{3,1},{4,2},{5,3},{6,4},{7,5},{8,14},{9,15},{10,... | collective-permute-start | bytes 2359304 | tf_op jit(solution)/shard_map/ppermute | solution.py:162
  400.3 30.4 %collective-permute-start.38 = (bf16[128,2048]{1,0:T(8,128)(2,1)S(1)}, bf16[128,2048]{1,0:T(8,128)(2,1)S(1)}, u32[]{:S(2)}, u32[]{:S(2)}) collective-permute-start(bf16[128,2048]{1,0:T(8,128)(2,1)S(1)} %slice.178), channel_id=1, source_target_pairs={{0,8},{8,16},{16,24},{24,0},{1,9},{9,17},{17,25},{25,1},{2,10},{10... | collective-permute-start | bytes 1572872 | tf_op jit(solution)/shard_map/ppermute | solution.py:162
  410.8 43.3 %collective-permute-start.23 = (bf16[192,2048]{1,0:T(8,128)(2,1)}, bf16[192,2048]{1,0:T(8,128)(2,1)}, u32[]{:S(2)}, u32[]{:S(2)}) collective-permute-start(bf16[192,2048]{1,0:T(8,128)(2,1)} %add_convert_fusion.refs_0_), channel_id=1, source_target_pairs={{0,1},{1,0},{2,3},{3,2},{4,5},{5,4},{6,7},{7,6},{8,9},{9,8},{10,11... | collective-permute-start | bytes 2359304 | tf_op jit(solution)/shard_map/ppermute | solution.py:243
  430.7 8.7 %collective-permute-start.28 = (bf16[96,2048]{1,0:T(8,128)(2,1)S(1)}, bf16[96,2048]{1,0:T(8,128)(2,1)S(1)}, u32[]{:S(2)}, u32[]{:S(2)}) collective-permute-start(bf16[96,2048]{1,0:T(8,128)(2,1)S(1)} %slice.174), channel_id=1, source_target_pairs={{0,2},{1,3},{2,4},{3,5},{4,6},{5,7},{6,0},{7,1},{8,10},{9,11},{10,... | collective-permute-start | bytes 1179656 | tf_op jit(solution)/shard_map/ppermute | solution.py:162
  431.8 15.1 %collective-permute-start.39 = (bf16[128,2048]{1,0:T(8,128)(2,1)}, bf16[128,2048]{1,0:T(8,128)(2,1)}, u32[]{:S(2)}, u32[]{:S(2)}) collective-permute-start(bf16[128,2048]{1,0:T(8,128)(2,1)} %slice.179), channel_id=1, source_target_pairs={{0,24},{8,0},{16,8},{24,16},{1,25},{9,1},{17,9},{25,17},{2,26},{10... | collective-permute-start | bytes 1572872 | tf_op jit(solution)/shard_map/ppermute | solution.py:162
  434.3 12.6 %collective-permute-start.42 = (bf16[256,1024]{1,0:T(8,128)(2,1)}, bf16[256,1024]{1,0:T(8,128)(2,1)}, u32[]{:S(2)}, u32[]{:S(2)}) collective-permute-start(bf16[256,1024]{1,0:T(8,128)(2,1)} %slice.180), channel_id=1, source_target_pairs={{0,8},{8,16},{16,24},{24,0},{1,9},{9,17},{17,25},{25,1},{2,10},{10... | collective-permute-start | bytes 1572872 | tf_op jit(solution)/shard_map/ppermute | solution.py:162
  435.6 18.5 %collective-permute-start.43 = (bf16[256,1024]{1,0:T(8,128)(2,1)}, bf16[256,1024]{1,0:T(8,128)(2,1)}, u32[]{:S(2)}, u32[]{:S(2)}) collective-permute-start(bf16[256,1024]{1,0:T(8,128)(2,1)} %slice.181), channel_id=1, source_target_pairs={{0,24},{8,0},{16,8},{24,16},{1,25},{9,1},{17,9},{25,17},{2,26},{10... | collective-permute-start | bytes 1572872 | tf_op jit(solution)/shard_map/ppermute | solution.py:162
  439.4 15.2 %collective-permute-start.30 = (bf16[96,2048]{1,0:T(8,128)(2,1)}, bf16[96,2048]{1,0:T(8,128)(2,1)}, u32[]{:S(2)}, u32[]{:S(2)}) collective-permute-start(bf16[96,2048]{1,0:T(8,128)(2,1)} %slice.175), channel_id=1, source_target_pairs={{0,6},{1,7},{2,0},{3,1},{4,2},{5,3},{6,4},{7,5},{8,14},{9,15},{10,... | collective-permute-start | bytes 1179656 | tf_op jit(solution)/shard_map/ppermute | solution.py:162
  446.9 10.8 %collective-permute-start.29 = (bf16[96,2048]{1,0:T(8,128)(2,1)S(1)}, bf16[96,2048]{1,0:T(8,128)(2,1)S(1)}, u32[]{:S(2)}, u32[]{:S(2)}) collective-permute-start(bf16[96,2048]{1,0:T(8,128)(2,1)S(1)} %collective-permute-done.28.refs_6_), channel_id=1, source_target_pairs={{0,1},{1,0},{2,3},{3,2},{4,5},{5,4},{6,7},{7,6},{8,9},{9,8},{10,11... | collective-permute-start | bytes 1179656 | tf_op jit(solution)/shard_map/ppermute | solution.py:243
  446.9 18.4 %collective-permute-start.25 = (bf16[192,2048]{1,0:T(8,128)(2,1)}, bf16[192,2048]{1,0:T(8,128)(2,1)}, u32[]{:S(2)}, u32[]{:S(2)}) collective-permute-start(bf16[192,2048]{1,0:T(8,128)(2,1)} %copy-done.15), channel_id=1, source_target_pairs={{0,1},{1,0},{2,3},{3,2},{4,5},{5,4},{6,7},{7,6},{8,9},{9,8},{10,11... | collective-permute-start | bytes 2359304 | tf_op jit(solution)/shard_map/ppermute | solution.py:243
  454.1 11.2 %collective-permute-start.27 = (bf16[192,2048]{1,0:T(8,128)(2,1)}, bf16[192,2048]{1,0:T(8,128)(2,1)}, u32[]{:S(2)}, u32[]{:S(2)}) collective-permute-start(bf16[192,2048]{1,0:T(8,128)(2,1)} %copy-done.16), channel_id=1, source_target_pairs={{0,1},{1,0},{2,3},{3,2},{4,5},{5,4},{6,7},{7,6},{8,9},{9,8},{10,11... | collective-permute-start | bytes 2359304 | tf_op jit(solution)/shard_map/ppermute | solution.py:243
  454.1 22.0 %collective-permute-start.32 = (bf16[192,2048]{1,0:T(8,128)(2,1)}, bf16[192,2048]{1,0:T(8,128)(2,1)}, u32[]{:S(2)}, u32[]{:S(2)}) collective-permute-start(bf16[192,2048]{1,0:T(8,128)(2,1)} %convert_element_type.224.refs_0_), channel_id=1, source_target_pairs={{0,8},{8,16},{16,24},{24,0},{1,9},{9,17},{17,25},{25,1},{2,10},{10... | collective-permute-start | bytes 2359304 | tf_op jit(solution)/shard_map/ppermute | solution.py:162
  454.6 22.7 %collective-permute-start.33 = (bf16[192,2048]{1,0:T(8,128)(2,1)}, bf16[192,2048]{1,0:T(8,128)(2,1)}, u32[]{:S(2)}, u32[]{:S(2)}) collective-permute-start(bf16[192,2048]{1,0:T(8,128)(2,1)} %convert_element_type.224.refs_0_), channel_id=1, source_target_pairs={{0,24},{8,0},{16,8},{24,16},{1,25},{9,1},{17,9},{25,17},{2,26},{10... | collective-permute-start | bytes 2359304 | tf_op jit(solution)/shard_map/ppermute | solution.py:162
  458.5 6.9 %collective-permute-start.31 = (bf16[96,2048]{1,0:T(8,128)(2,1)}, bf16[96,2048]{1,0:T(8,128)(2,1)}, u32[]{:S(2)}, u32[]{:S(2)}) collective-permute-start(bf16[96,2048]{1,0:T(8,128)(2,1)} %collective-permute-done.30.refs_8_), channel_id=1, source_target_pairs={{0,1},{1,0},{2,3},{3,2},{4,5},{5,4},{6,7},{7,6},{8,9},{9,8},{10,11... | collective-permute-start | bytes 1179656 | tf_op jit(solution)/shard_map/ppermute | solution.py:243
  472.0 10.6 %collective-permute-start.44 = (bf16[64,2048]{1,0:T(8,128)(2,1)S(1)}, bf16[64,2048]{1,0:T(8,128)(2,1)}, u32[]{:S(2)}, u32[]{:S(2)}) collective-permute-start(bf16[64,2048]{1,0:T(8,128)(2,1)S(1)} %convert_element_type.225.refs_0_), channel_id=1, source_target_pairs={{0,8},{8,16},{16,24},{24,0},{1,9},{9,17},{17,25},{25,1},{2,10},{10... | collective-permute-start | bytes 786440 | tf_op jit(solution)/shard_map/ppermute | solution.py:162
  477.1 13.8 %collective-permute-start.34 = (bf16[96,2048]{1,0:T(8,128)(2,1)S(1)}, bf16[96,2048]{1,0:T(8,128)(2,1)}, u32[]{:S(2)}, u32[]{:S(2)}) collective-permute-start(bf16[96,2048]{1,0:T(8,128)(2,1)S(1)} %slice.176), channel_id=1, source_target_pairs={{0,8},{8,16},{16,24},{24,0},{1,9},{9,17},{17,25},{25,1},{2,10},{10... | collective-permute-start | bytes 1179656 | tf_op jit(solution)/shard_map/ppermute | solution.py:162
  478.3 12.8 %collective-permute-start.35 = (bf16[96,2048]{1,0:T(8,128)(2,1)S(1)}, bf16[96,2048]{1,0:T(8,128)(2,1)}, u32[]{:S(2)}, u32[]{:S(2)}) collective-permute-start(bf16[96,2048]{1,0:T(8,128)(2,1)S(1)} %slice.177), channel_id=1, source_target_pairs={{0,24},{8,0},{16,8},{24,16},{1,25},{9,1},{17,9},{25,17},{2,26},{10... | collective-permute-start | bytes 1179656 | tf_op jit(solution)/shard_map/ppermute | solution.py:162
  481.6 13.8 %collective-permute-start.45 = (bf16[64,2048]{1,0:T(8,128)(2,1)S(1)}, bf16[64,2048]{1,0:T(8,128)(2,1)}, u32[]{:S(2)}, u32[]{:S(2)}) collective-permute-start(bf16[64,2048]{1,0:T(8,128)(2,1)S(1)} %convert_element_type.225.refs_0_), channel_id=1, source_target_pairs={{0,24},{8,0},{16,8},{24,16},{1,25},{9,1},{17,9},{25,17},{2,26},{10... | collective-permute-start | bytes 786440 | tf_op jit(solution)/shard_map/ppermute | solution.py:162
  482.6 13.4 %collective-permute-start.46 = (bf16[64,2048]{1,0:T(8,128)(2,1)}, bf16[64,2048]{1,0:T(8,128)(2,1)}, u32[]{:S(2)}, u32[]{:S(2)}) collective-permute-start(bf16[64,2048]{1,0:T(8,128)(2,1)} %collective-permute-done.44.refs_1_), channel_id=1, source_target_pairs={{0,8},{8,16},{16,24},{24,0},{1,9},{9,17},{17,25},{25,1},{2,10},{10... | collective-permute-start | bytes 786440 | tf_op jit(solution)/shard_map/ppermute | solution.py:162
  (43 other events, 487.6 us)
Sparse Core Ops, SparseCore 0:
  30.3 80.7 reduce-scatter.3
  203.0 105.3 reduce-scatter.5
  355.8 45.0 reduce-scatter.7
